TPU v7x, 16 devices: a whole 2x2x2 slice. The times are simulated.
16 devices in a mesh: depth: 2 (over z), col: 2 (over y), row: 4 (over x, core).
Axes of the slice: x: 2, y: 2, z: 2, core: 2. Of those that a mesh axis runs over, the one named last changes fastest.
Arguments:
- a_mat: bfloat16 [8192, 8192], P('row', 'col')
- b_mat: bfloat16 [8192, 8192], P('row', 'col')
Outputs:
- output: bfloat16 [8192, 8192], P(('row', 'depth'), 'col')
All inputs are finite; a program needn't handle non-finite values.
Results may differ from a plain program's by a relative error of at most 0.001.
Values are sent between devices in bfloat16 or wider.
A program may use at most 1 GiB of HBM per device.

v0:
```python
import jax
import jax.numpy as jnp
from jax import lax
from jax.sharding import PartitionSpec as P

AXES_ALL = ("depth", "col", "row")


def skew_pairs(depth_n, col_n, row_n):
    col_ratio = row_n // col_n
    layer_steps = row_n // depth_n
    pairs_a0 = []
    pairs_a1 = []
    pairs_b = []
    for layer_idx in range(depth_n):
        for col_idx in range(col_n):
            for row_idx in range(row_n):
                target_dev = (layer_idx * col_n + col_idx) * row_n + row_idx
                start_blk = (row_idx + col_ratio * col_idx + layer_idx * layer_steps) % row_n
                coarse_blk = start_blk // col_ratio
                pairs_a0.append(((layer_idx * col_n + coarse_blk) * row_n + row_idx, target_dev))
                pairs_a1.append(((layer_idx * col_n + (coarse_blk + 1) % col_n) * row_n + row_idx, target_dev))
                pairs_b.append(((layer_idx * col_n + col_idx) * row_n + start_blk, target_dev))
    return pairs_a0, pairs_a1, pairs_b


def solution(mesh):
    depth_n = mesh.shape["depth"]
    col_n = mesh.shape["col"]
    row_n = mesh.shape["row"]
    col_ratio = row_n // col_n
    layer_steps = row_n // depth_n
    pairs_a0, pairs_a1, pairs_b = skew_pairs(depth_n, col_n, row_n)
    pairs_col = [((col_idx + 1) % col_n, col_idx) for col_idx in range(col_n)]
    pairs_row = [((row_idx + 1) % row_n, row_idx) for row_idx in range(row_n)]

    def local_mm(a_blk, b_blk):
        layer_idx = lax.axis_index("depth")
        row_idx = lax.axis_index("row")
        fine_side = a_blk.shape[0]
        a_first = lax.ppermute(a_blk, AXES_ALL, pairs_a0)
        if col_ratio > 1:
            a_second = lax.ppermute(a_blk, AXES_ALL, pairs_a1)
            a_joined = jnp.concatenate([a_first, a_second], axis=1)
            offset = ((row_idx + layer_idx * layer_steps) % col_ratio) * fine_side
            a_window = lax.dynamic_slice_in_dim(a_joined, offset, a_blk.shape[1], axis=1)
        else:
            a_window = a_first
        a_parts = [a_window[:, blk_idx * fine_side:(blk_idx + 1) * fine_side] for blk_idx in range(min(col_ratio, layer_steps))]
        b_cur = lax.ppermute(b_blk, AXES_ALL, pairs_b)
        part_sum = None
        for step_idx in range(layer_steps):
            a_cur = a_parts[step_idx]
            block_prod = jnp.dot(a_cur, b_cur, preferred_element_type=jnp.float32)
            part_sum = block_prod if part_sum is None else part_sum + block_prod
            if step_idx + col_ratio < layer_steps:
                a_parts.append(lax.ppermute(a_cur, "col", pairs_col))
            if step_idx + 1 < layer_steps:
                b_cur = lax.ppermute(b_cur, "row", pairs_row)
        c_rows = lax.psum_scatter(part_sum, "depth", scatter_dimension=0, tiled=True)
        return c_rows.astype(jnp.bfloat16)

    spec_in = P("row", "col")
    spec_out = P(("row", "depth"), "col")
    return jax.shard_map(local_mm, mesh=mesh, in_specs=(spec_in, spec_in), out_specs=spec_out, check_vma=False)
```

profile of v0, /device:TPU:0, one launch (start us, length us, event | category | flops | bytes accessed | tf_op | source)
XLA Modules:
  0.0 1116.1 jit_solution(9805907198922978389)
XLA Ops:
  6.5 0.0 reduce-scatter.2.cloned.1.call-start
  6.5 127.3 %collective-permute-start.2 = (bf16[2048,4096]{1,0:T(8,128)(2,1)}, bf16[2048,4096]{1,0:T(8,128)(2,1)}, u32[]{:S(2)}, u32[]{:S(2)}) collective-permute-start(bf16[2048,4096]{1,0:T(8,128)(2,1)} %param.3), channel_id=1, source_target_pairs={{0,0},{1,1},{2,2},{3,3},{6,4},{7,5},{4,6},{5,7},{10,8},{11,9},{8,1... | collective-permute-start | bytes 50331656 | tf_op jit(solution)/shard_map/ppermute | solution.py:50
  133.9 1.9 collective-permute-start.1
  135.8 127.4 %collective-permute-start = (bf16[2048,4096]{1,0:T(8,128)(2,1)}, bf16[2048,4096]{1,0:T(8,128)(2,1)}, u32[]{:S(2)}, u32[]{:S(2)}) collective-permute-start(bf16[2048,4096]{1,0:T(8,128)(2,1)} %param.2), channel_id=1, source_target_pairs={{0,0},{1,1},{6,2},{7,3},{4,4},{5,5},{2,6},{3,7},{12,8},{13,9},{10,... | collective-permute-start | bytes 50331656 | tf_op jit(solution)/shard_map/ppermute | solution.py:41
  263.1 0.0 collective-permute-done.2
  263.1 2.7 collective-permute-start.3
  265.8 232.8 %collective-permute-done.1 = bf16[2048,4096]{1,0:T(8,128)(2,1)} collective-permute-done((bf16[2048,4096]{1,0:T(8,128)(2,1)}, bf16[2048,4096]{1,0:T(8,128)(2,1)}, u32[]{:S(2)}, u32[]{:S(2)}) %collective-permute-start.1) | collective-permute-done | bytes 16777248 | tf_op jit(solution)/shard_map/ppermute | solution.py:43
  498.6 0.0 collective-permute-done
  498.6 16.6 %fusion = bf16[2048,4096]{1,0:T(8,128)(2,1)} fusion(s32[]{:T(128)S(6)} %select_n.11, bf16[2048,4096]{1,0:T(8,128)(2,1)} %collective-permute-done, bf16[2048,4096]{1,0:T(8,128)(2,1)} %collective-permute-done.1), kind=kLoop, calls=%fused_computation.3 | loop fusion | flops 33554432 | bytes 50331652 | tf_op jit(solution)/shard_map/concatenate | solution.py:44
  515.2 43.5 %fusion.2 = f32[2048,4096]{1,0:T(8,128)} fusion(bf16[2048,4096]{1,0:T(8,128)(2,1)} %collective-permute-done.2, bf16[2048,4096]{1,0:T(8,128)(2,1)} %fusion), kind=kOutput, calls=%fused_computation.5 | convolution fusion | flops 34359738368 | bytes 58720256 | tf_op jit(solution)/shard_map/dot_general | solution.py:54
  558.7 0.0 collective-permute-done.3
  558.7 46.1 %convolution_add_fusion = f32[2048,4096]{1,0:T(8,128)} fusion(f32[2048,4096]{1,0:T(8,128)} %fusion.2, bf16[2048,4096]{1,0:T(8,128)(2,1)} %collective-permute-done.3, bf16[2048,4096]{1,0:T(8,128)(2,1)} %fusion), kind=kOutput, calls=%fused_computation.2 | convolution fusion | flops 34368126976 | bytes 92274688 | tf_op jit(solution)/shard_map/dot_general | solution.py:54
  604.8 0.0 reduce-scatter.2.cloned.1.call-update
  604.9 495.5 %reduce-scatter.2.cloned.1.call-done = f32[1024,4096]{1,0:T(8,128)} async-done(((f32[2048,4096]{1,0:T(8,128)}), f32[1024,4096]{1,0:T(8,128)}) %reduce-scatter.2.cloned.1.call-update) | async-done | bytes 16777232 | tf_op jit(solution)/shard_map/reduce_scatter | solution.py:60
  1100.3 9.0 convert_element_type.3
Async XLA Ops:
  6.5 1093.8 %reduce-scatter.2.cloned.1.call-start = ((), (), s32[]{:S(2)}) async-start(), calls=%async_computation.1 | async-start | bytes 50331648 | tf_op jit(solution)/shard_map/reduce_scatter | solution.py:60
  6.5 256.6 %collective-permute-start.2 = (bf16[2048,4096]{1,0:T(8,128)(2,1)}, bf16[2048,4096]{1,0:T(8,128)(2,1)}, u32[]{:S(2)}, u32[]{:S(2)}) collective-permute-start(bf16[2048,4096]{1,0:T(8,128)(2,1)} %param.3), channel_id=1, source_target_pairs={{0,0},{1,1},{2,2},{3,3},{6,4},{7,5},{4,6},{5,7},{10,8},{11,9},{8,1... | collective-permute-start | bytes 50331656 | tf_op jit(solution)/shard_map/ppermute | solution.py:50
  133.9 364.8 %collective-permute-start.1 = (bf16[2048,4096]{1,0:T(8,128)(2,1)}, bf16[2048,4096]{1,0:T(8,128)(2,1)}, u32[]{:S(2)}, u32[]{:S(2)}) collective-permute-start(bf16[2048,4096]{1,0:T(8,128)(2,1)} %param.2), channel_id=1, source_target_pairs={{4,0},{5,1},{2,2},{3,3},{0,4},{1,5},{6,6},{7,7},{8,8},{9,9},{14,10... | collective-permute-start | bytes 50331656 | tf_op jit(solution)/shard_map/ppermute | solution.py:43
  135.8 362.8 %collective-permute-start = (bf16[2048,4096]{1,0:T(8,128)(2,1)}, bf16[2048,4096]{1,0:T(8,128)(2,1)}, u32[]{:S(2)}, u32[]{:S(2)}) collective-permute-start(bf16[2048,4096]{1,0:T(8,128)(2,1)} %param.2), channel_id=1, source_target_pairs={{0,0},{1,1},{6,2},{7,3},{4,4},{5,5},{2,6},{3,7},{12,8},{13,9},{10,... | collective-permute-start | bytes 50331656 | tf_op jit(solution)/shard_map/ppermute | solution.py:41
  263.1 295.6 %collective-permute-start.3 = (bf16[2048,4096]{1,0:T(8,128)(2,1)}, bf16[2048,4096]{1,0:T(8,128)(2,1)}, u32[]{:S(2)}, u32[]{:S(2)}) collective-permute-start(bf16[2048,4096]{1,0:T(8,128)(2,1)} %collective-permute-done.2), channel_id=1, source_target_pairs={{1,0},{2,1},{3,2},{0,3},{5,4},{6,5},{7,6},{4,7},{9,8},{10,9},{11,1... | collective-permute-start | bytes 50331656 | tf_op jit(solution)/shard_map/ppermute | solution.py:59
Sparse Core Ops, SparseCore 0:
  605.0 495.3 reduce-scatter.1
where the time goes:
time: 1130 us; the launch traced here: 1120 us
  waiting for transfers between devices  728 us (64%)
  starting transfers between devices  259 us (23%)
  matrix products  89.6 us (8%)
  other arithmetic  25.6 us (2%)
  between operations  13.4 us (1%)
    reduce_scatter x1, waiting for transfers between devices, local_mm(): lax.psum_scatter(part_sum, 'depth', scatter_dimension=0, tiled=True)  495 us
    ppermute x1, waiting for transfers between devices, local_mm(): a_second = lax.ppermute(a_blk, AXES_ALL, pairs_a1)  233 us
    ppermute x1, starting transfers between devices, local_mm(): a_first = lax.ppermute(a_blk, AXES_ALL, pairs_a0)  127 us
    ppermute x1, starting transfers between devices, local_mm(): b_cur = lax.ppermute(b_blk, AXES_ALL, pairs_b)  127 us
    dot_general x2, matrix products, local_mm(): block_prod = jnp.dot(a_cur, b_cur, preferred_element_type=jnp.float32)  89.6 us
  transfers between devices with their start and end apart: 5, of which 2 were waited for; matrix products, arithmetic and copies ran while one was open for 5% of the time, Pallas kernels for 0%

commit v1 on v0

v1 whole, which is shorter than its diff:
```python
import functools

import jax
import jax.numpy as jnp
from jax import lax
from jax.experimental import pallas as pl
from jax.experimental.pallas import tpu as pltpu
from jax.sharding import PartitionSpec as P

MESH = pl.DeviceIdType.MESH
GROUP = 128
SUBS = 4
AHEAD = 8
LAG = 3
TILE = 512


def kernel(a_ref, b_ref, c_ref, ball, a_v, acc, b_far, b_near, o_v,
           load_a, send_a, recv_a, send_x, recv_x, send_z, recv_z, send_own, recv_own,
           send_px, recv_px, send_pz, recv_pz, load_far, load_near, store_c):
    depth = lax.axis_index("depth")
    col = lax.axis_index("col")
    row = lax.axis_index("row")
    core = lax.rem(row, 2)
    chip_x = row // 2
    rows_c = a_ref.shape[0] // 2
    band = b_ref.shape[0]
    cols = b_ref.shape[1]
    steps = band // GROUP
    half = cols // 2
    width = half // SUBS
    count = steps * SUBS
    quarter = cols // SUBS

    row_far = lax.rem(row + 2, 4)
    row_peer = chip_x * 2 + (1 - core)
    row_far_peer = lax.rem(row_peer + 2, 4)
    dev_x = (depth, col, row_far)
    dev_y = (depth, 1 - col, row)
    dev_z = (1 - depth, col, row)
    dev_p = (depth, col, row_peer)
    at_near = chip_x * steps
    at_far = (1 - chip_x) * steps
    at_mine = col * steps
    at_other = (1 - col) * steps

    def a_load(step, part):
        return pltpu.make_async_copy(
            a_ref.at[pl.ds(depth * rows_c, rows_c), pl.ds(part * band + step * GROUP, GROUP)],
            a_v.at[at_mine + step, :, pl.ds(part * GROUP, GROUP)],
            load_a.at[step])

    def a_load_wait(step):
        pltpu.make_async_copy(a_v.at[at_mine + step], a_v.at[at_mine + step], load_a.at[step]).wait()

    def a_send(step):
        return pltpu.make_async_remote_copy(
            a_v.at[at_mine + step], a_v.at[at_mine + step], send_a.at[step], recv_a.at[step],
            device_id=dev_y, device_id_type=MESH)

    def a_recv(step):
        return pltpu.make_async_remote_copy(
            a_v.at[at_other + step], a_v.at[at_other + step], send_a.at[step], recv_a.at[step],
            device_id=dev_y, device_id_type=MESH)

    def piece(band_row, num, which):
        step = num // SUBS
        sub = lax.rem(num, SUBS)
        return ball.at[pl.ds(band_row * band + step * GROUP, GROUP), pl.ds(which * half + sub * width, width)]

    def x_send(num):
        step = num // SUBS
        sub = lax.rem(num, SUBS)
        return pltpu.make_async_remote_copy(
            b_ref.at[pl.ds(step * GROUP, GROUP), pl.ds(depth * half + sub * width, width)],
            piece(row, num, depth), send_x.at[num], recv_x.at[num], device_id=dev_x, device_id_type=MESH)

    def x_recv(num):
        return pltpu.make_async_remote_copy(
            piece(row_far, num, depth), piece(row_far, num, depth), send_x.at[num], recv_x.at[num],
            device_id=dev_x, device_id_type=MESH)

    def z_send(num):
        return pltpu.make_async_remote_copy(
            piece(row_far, num, depth), piece(row_far, num, depth), send_z.at[num], recv_z.at[num],
            device_id=dev_z, device_id_type=MESH)

    def z_recv(num):
        return pltpu.make_async_remote_copy(
            piece(row_far, num, 1 - depth), piece(row_far, num, 1 - depth), send_z.at[num], recv_z.at[num],
            device_id=dev_z, device_id_type=MESH)

    def own_send(step):
        return pltpu.make_async_remote_copy(
            b_ref.at[pl.ds(step * GROUP, GROUP), :], ball.at[pl.ds(row * band + step * GROUP, GROUP), :],
            send_own.at[step], recv_own.at[step], device_id=dev_p, device_id_type=MESH)

    def own_recv(step):
        here = ball.at[pl.ds(row_peer * band + step * GROUP, GROUP), :]
        return pltpu.make_async_remote_copy(
            here, here, send_own.at[step], recv_own.at[step], device_id=dev_p, device_id_type=MESH)

    def half_group(band_row, step, which):
        return ball.at[pl.ds(band_row * band + step * GROUP, GROUP), pl.ds(which * half, half)]

    def px_send(step):
        here = half_group(row_far, step, depth)
        return pltpu.make_async_remote_copy(
            here, here, send_px.at[step], recv_px.at[step], device_id=dev_p, device_id_type=MESH)

    def px_recv(step):
        here = half_group(row_far_peer, step, depth)
        return pltpu.make_async_remote_copy(
            here, here, send_px.at[step], recv_px.at[step], device_id=dev_p, device_id_type=MESH)

    def pz_send(num):
        here = piece(row_far, num, 1 - depth)
        return pltpu.make_async_remote_copy(
            here, here, send_pz.at[num], recv_pz.at[num], device_id=dev_p, device_id_type=MESH)

    def pz_recv(num):
        here = piece(row_far_peer, num, 1 - depth)
        return pltpu.make_async_remote_copy(
            here, here, send_pz.at[num], recv_pz.at[num], device_id=dev_p, device_id_type=MESH)

    def near_loads(step):
        slot = lax.rem(step, 2)
        pltpu.make_async_copy(
            b_ref.at[pl.ds(step * GROUP, GROUP), :],
            b_near.at[slot, pl.ds(core * GROUP, GROUP), :], load_near.at[slot]).start()
        pltpu.make_async_copy(
            ball.at[pl.ds(row_peer * band + step * GROUP, GROUP), :],
            b_near.at[slot, pl.ds((1 - core) * GROUP, GROUP), :], load_near.at[slot]).start()

    def near_wait(step):
        slot = lax.rem(step, 2)
        pltpu.make_async_copy(b_near.at[slot], b_near.at[slot], load_near.at[slot]).wait()

    def far_loads(step):
        slot = lax.rem(step, 2)
        pltpu.make_async_copy(
            ball.at[pl.ds(row_far * band + step * GROUP, GROUP), :],
            b_far.at[slot, pl.ds(core * GROUP, GROUP), :], load_far.at[slot]).start()
        pltpu.make_async_copy(
            ball.at[pl.ds(row_far_peer * band + step * GROUP, GROUP), :],
            b_far.at[slot, pl.ds((1 - core) * GROUP, GROUP), :], load_far.at[slot]).start()

    def far_wait(step):
        slot = lax.rem(step, 2)
        pltpu.make_async_copy(b_far.at[slot], b_far.at[slot], load_far.at[slot]).wait()

    def add(a_at, buf, slot, sub):
        @pl.loop(0, quarter // TILE)
        def _(tile):
            at = pl.ds(pl.multiple_of(sub * quarter + tile * TILE, TILE), TILE)
            acc[:, at] += jnp.dot(a_v[a_at], buf[slot, :, at], preferred_element_type=jnp.float32)

    @pl.loop(0, steps)
    def _(step):
        a_load(step, 0).start()
        a_load(step, 1).start()

    barrier = pltpu.get_barrier_semaphore()
    for dev in (dev_x, dev_y, dev_z, dev_p):
        pl.semaphore_signal(barrier, inc=1, device_id=dev, device_id_type=MESH)
    pl.semaphore_wait(barrier, 4)

    @pl.loop(0, AHEAD)
    def _(num):
        x_send(num).start()

    own_send(0).start()
    own_send(1).start()

    @pl.loop(0, steps)
    def _(step):
        a_load_wait(step)
        a_send(step).start()

    @pl.loop(0, cols // TILE)
    def _(tile):
        at = pl.ds(pl.multiple_of(tile * TILE, TILE), TILE)
        acc[:, at] = jnp.zeros((rows_c, TILE), jnp.float32)

    @pl.loop(0, count)
    def _(num):
        step = num // SUBS
        sub = lax.rem(num, SUBS)
        x_recv(num).wait_recv()
        z_send(num).start()

        @pl.when(num + AHEAD < count)
        def _():
            x_send(num + AHEAD).start()

        @pl.when(sub == SUBS - 1)
        def _():
            px_send(step).start()

        @pl.when(num >= LAG)
        def _():
            z_recv(num - LAG).wait_recv()
            pz_send(num - LAG).start()

        @pl.when(sub == 0)
        def _():
            own_recv(step).wait_recv()
            near_loads(step)

            @pl.when(step + 2 < steps)
            def _():
                own_send(step + 2).start()

            @pl.when(step >= 1)
            def _():
                a_recv(step - 1).wait_recv()
                near_wait(step - 1)

            @pl.when(step >= 2)
            def _():
                far_wait(step - 2)

        @pl.when(step >= 1)
        def _():
            add(at_near + step - 1, b_near, lax.rem(step - 1, 2), sub)

        @pl.when(step >= 2)
        def _():
            add(at_far + step - 2, b_far, lax.rem(step - 2, 2), sub)

        @pl.when((sub == SUBS - 1) & (step >= 1))
        def _():
            px_recv(step - 1).wait_recv()
            for k in range(SUBS):
                pz_recv((step - 1) * SUBS + k).wait_recv()
            far_loads(step - 1)

    last = steps - 1
    a_recv(last).wait_recv()
    near_wait(last)
    far_wait(last - 1)

    for k in range(SUBS):
        if k < LAG:
            z_recv(count - LAG + k).wait_recv()
            pz_send(count - LAG + k).start()
        add(at_near + last, b_near, last % 2, k)
        add(at_far + last - 1, b_far, (last - 1) % 2, k)

    px_recv(last).wait_recv()
    for k in range(SUBS):
        pz_recv(last * SUBS + k).wait_recv()
    far_loads(last)
    far_wait(last)

    def c_store(sub):
        at = pl.ds(pl.multiple_of(sub * quarter, quarter), quarter)
        return pltpu.make_async_copy(o_v.at[:, at], c_ref.at[:, at], store_c.at[sub])

    @pl.loop(0, SUBS)
    def _(sub):
        @pl.loop(0, quarter // TILE)
        def _(tile):
            at = pl.ds(pl.multiple_of(sub * quarter + tile * TILE, TILE), TILE)
            total = acc[:, at] + jnp.dot(
                a_v[at_far + last], b_far[last % 2, :, at], preferred_element_type=jnp.float32)
            o_v[:, at] = total.astype(o_v.dtype)
        c_store(sub).start()

    @pl.loop(0, count)
    def _(num):
        x_send(num).wait_send()
        z_send(num).wait_send()
        pz_send(num).wait_send()

    @pl.loop(0, steps)
    def _(step):
        a_send(step).wait_send()
        own_send(step).wait_send()
        px_send(step).wait_send()

    @pl.loop(0, SUBS)
    def _(sub):
        c_store(sub).wait()


def solution(mesh):
    def local_mm(a_blk, b_blk):
        band, cols = b_blk.shape
        rows_c = a_blk.shape[0] // 2
        steps = band // GROUP
        count = steps * SUBS
        any_spec = pl.BlockSpec(memory_space=pl.ANY)
        dma = pltpu.SemaphoreType.DMA
        c_blk, _ = pl.pallas_call(
            kernel,
            out_shape=(jax.ShapeDtypeStruct((rows_c, cols), jnp.bfloat16),
                       jax.ShapeDtypeStruct((4 * band, cols), jnp.bfloat16)),
            in_specs=[any_spec] * 2,
            out_specs=(any_spec, any_spec),
            scratch_shapes=[
                pltpu.VMEM((2 * steps, rows_c, 2 * GROUP), jnp.bfloat16),
                pltpu.VMEM((rows_c, cols), jnp.float32),
                pltpu.VMEM((2, 2 * GROUP, cols), jnp.bfloat16),
                pltpu.VMEM((2, 2 * GROUP, cols), jnp.bfloat16),
                pltpu.VMEM((rows_c, cols), jnp.bfloat16),
                dma((steps,)), dma((steps,)), dma((steps,)),
                dma((count,)), dma((count,)), dma((count,)), dma((count,)),
                dma((steps,)), dma((steps,)), dma((steps,)), dma((steps,)),
                dma((count,)), dma((count,)),
                dma((2,)), dma((2,)), dma((SUBS,)),
            ],
            compiler_params=pltpu.CompilerParams(
                collective_id=0, has_side_effects=True, vmem_limit_bytes=60 * 1024 * 1024),
            cost_estimate=pl.CostEstimate(
                flops=2 * rows_c * cols * 2 * cols, bytes_accessed=200 * 2 ** 20, transcendentals=0),
        )(a_blk, b_blk)
        return c_blk

    return jax.shard_map(
        local_mm, mesh=mesh, in_specs=(P("row", "col"), P("row", "col")),
        out_specs=P(("row", "depth"), "col"), check_vma=False)
```

time: 1130 us -> 215 us (0.19); the launches traced: 1120 us -> 214 us
  waiting for transfers between devices: 728 us -> 0 us
  starting transfers between devices: 259 us -> 0 us
  Pallas kernels: 0 us -> 207 us
  matrix products: 89.6 us -> 0 us
  other arithmetic: 25.6 us -> 0 us
  between operations: 13.4 us -> 0.01 us
    reduce_scatter x1 -> x0, waiting for transfers between devices: 495 us -> none  [local_mm(): lax.psum_scatter(part_sum, 'depth', scatter_dimension=0, tiled=True)]
    ppermute x4 -> x0, starting transfers between devices: 259 us -> none  [the longest x1 127 us: local_mm(): a_first = lax.ppermute(a_blk, AXES_ALL, pairs_a0)]
    ppermute x4 -> x0, waiting for transfers between devices: 233 us -> none  [the longest x1 233 us: local_mm(): a_second = lax.ppermute(a_blk, AXES_ALL, pairs_a1)]
    pallas_call x0 -> x1, Pallas kernels: none -> 207 us  [local_mm(): pl.pallas_call(kernel, out_shape=(jax.ShapeDtypeStruct((rows_c, cols), jn...]
    dot_general x2 -> x0, matrix products: 89.6 us -> none  [local_mm(): block_prod = jnp.dot(a_cur, b_cur, preferred_element_type=jnp.float32)]
    concatenate x1 -> x0, other arithmetic: 16.6 us -> none  [local_mm(): a_joined = jnp.concatenate([a_first, a_second], axis=1)]
  transfers between devices with their start and end apart: 5 -> 0, of which waited for: 2 -> 0; matrix products, arithmetic and copies ran while one was open for 5% -> 0% of each run, Pallas kernels for 0% -> 0%
where the time goes in v1:
time: 215 us; the launch traced here: 214 us
  Pallas kernels  207 us (96%)
  local copies, waits for them, and re-layouts  7.89 us (4%)
    pallas_call x1, Pallas kernels, local_mm(): pl.pallas_call(kernel, out_shape=(jax.ShapeDtypeStruct((rows_c, cols), jn...  207 us
    unnamed x1, local copies, waits for them, and re-layouts  7.89 us

profile of v1, /device:TPU:0, one launch (start us, length us, event | category | flops | bytes accessed | tf_op | source)
XLA Modules:
  0.0 214.4 jit_solution(8542932097151196162)
XLA Ops:
  0.0 206.6 %shard_map.28 = (bf16[1024,4096]{1,0:T(8,128)(2,1)}, bf16[8192,4096]{1,0:T(8,128)(2,1)}) custom-call(bf16[2048,4096]{1,0:T(8,128)(2,1)} %a_ref.1, bf16[2048,4096]{1,0:T(8,128)(2,1)} %b_ref.1), custom_call_target="tpu_custom_call" | custom-call | flops 68719476736 | bytes 209715200 | tf_op jit(solution)/shard_map/pallas_call | solution.py:295
  206.6 7.9 %copy.4 = bf16[1024,4096]{1,0:T(8,128)(2,1)} copy(bf16[1024,4096]{1,0:T(8,128)(2,1)} %get-tuple-element.6) | data formatting | bytes 16777216

commit v2 on v1

v2 whole, which is shorter than its diff:
```python
import functools

import jax
import jax.numpy as jnp
from jax import lax
from jax.experimental import pallas as pl
from jax.experimental.pallas import tpu as pltpu
from jax.sharding import PartitionSpec as P

MESH = pl.DeviceIdType.MESH
GROUP = 128
SUBS = 8
AHEAD = 12
LAG = 4
SHIFT = 2
FAR = SUBS + LAG + 2
TILE = 512


def kernel(a_ref, b_ref, o_v, ball, a_v, acc, b_far, b_near, b_last,
           load_a, send_a, recv_a, send_x, recv_x, send_z, recv_z, send_own, recv_own,
           send_px, recv_px, send_pz, recv_pz, load_far, load_near, send_pl, recv_pl):
    depth = lax.axis_index("depth")
    col = lax.axis_index("col")
    row = lax.axis_index("row")
    core = lax.rem(row, 2)
    chip_x = row // 2
    rows_c = a_ref.shape[0] // 2
    band = b_ref.shape[0]
    cols = b_ref.shape[1]
    steps = band // GROUP
    half = cols // 2
    width = half // SUBS
    count = steps * SUBS

    row_far = lax.rem(row + 2, 4)
    row_peer = chip_x * 2 + (1 - core)
    row_far_peer = lax.rem(row_peer + 2, 4)
    dev_x = (depth, col, row_far)
    dev_y = (depth, 1 - col, row)
    dev_z = (1 - depth, col, row)
    dev_p = (depth, col, row_peer)
    at_near = chip_x * steps
    at_far = (1 - chip_x) * steps
    at_mine = col * steps
    at_other = (1 - col) * steps

    def a_load(step, part):
        return pltpu.make_async_copy(
            a_ref.at[pl.ds(depth * rows_c, rows_c), pl.ds(part * band + step * GROUP, GROUP)],
            a_v.at[at_mine + step, :, pl.ds(part * GROUP, GROUP)],
            load_a.at[step])

    def a_load_wait(step):
        pltpu.make_async_copy(a_v.at[at_mine + step], a_v.at[at_mine + step], load_a.at[step]).wait()

    def a_send(step):
        return pltpu.make_async_remote_copy(
            a_v.at[at_mine + step], a_v.at[at_mine + step], send_a.at[step], recv_a.at[step],
            device_id=dev_y, device_id_type=MESH)

    def a_recv(step):
        return pltpu.make_async_remote_copy(
            a_v.at[at_other + step], a_v.at[at_other + step], send_a.at[step], recv_a.at[step],
            device_id=dev_y, device_id_type=MESH)

    def piece(band_row, num, which):
        step = num // SUBS
        sub = lax.rem(num, SUBS)
        return ball.at[pl.ds(band_row * band + step * GROUP, GROUP), pl.ds(which * half + sub * width, width)]

    def last_piece(core_of, num, which):
        return b_last.at[pl.ds(core_of * GROUP, GROUP), pl.ds(which * half + lax.rem(num, SUBS) * width, width)]

    def source(num, which):
        return b_ref.at[pl.ds((num // SUBS) * GROUP, GROUP),
                        pl.ds(which * half + lax.rem(num, SUBS) * width, width)]

    def remote(src, dst, send, recv, num, dev):
        return pltpu.make_async_remote_copy(
            src, dst, send.at[num], recv.at[num], device_id=dev, device_id_type=MESH)

    def x_send(num):
        return remote(source(num, depth), piece(row, num, depth), send_x, recv_x, num, dev_x)

    def x_send_last(num):
        return remote(source(num, depth), last_piece(core, num, depth), send_x, recv_x, num, dev_x)

    def x_send_extra(num):
        return remote(source(num, 1 - depth), last_piece(core, num, 1 - depth), send_z, recv_z, num, dev_x)

    def x_recv(num):
        here = piece(row_far, num, depth)
        return remote(here, here, send_x, recv_x, num, dev_x)

    def x_recv_last(num):
        here = last_piece(core, num, depth)
        return remote(here, here, send_x, recv_x, num, dev_x)

    def z_send(num):
        here = piece(row_far, num, depth)
        return remote(here, here, send_z, recv_z, num, dev_z)

    def z_send_last(num):
        here = last_piece(core, num, depth)
        return remote(here, here, send_z, recv_z, num, dev_z)

    def z_recv(num):
        here = piece(row_far, num, 1 - depth)
        return remote(here, here, send_z, recv_z, num, dev_z)

    def z_recv_last(num):
        here = last_piece(core, num, 1 - depth)
        return remote(here, here, send_z, recv_z, num, dev_z)

    def own_send(step):
        return pltpu.make_async_remote_copy(
            b_ref.at[pl.ds(step * GROUP, GROUP), :], ball.at[pl.ds(row * band + step * GROUP, GROUP), :],
            send_own.at[step], recv_own.at[step], device_id=dev_p, device_id_type=MESH)

    def own_recv(step):
        here = ball.at[pl.ds(row_peer * band + step * GROUP, GROUP), :]
        return pltpu.make_async_remote_copy(
            here, here, send_own.at[step], recv_own.at[step], device_id=dev_p, device_id_type=MESH)

    def half_group(band_row, step, which):
        return ball.at[pl.ds(band_row * band + step * GROUP, GROUP), pl.ds(which * half, half)]

    def px_send(step):
        here = half_group(row_far, step, depth)
        return pltpu.make_async_remote_copy(
            here, here, send_px.at[step], recv_px.at[step], device_id=dev_p, device_id_type=MESH)

    def px_recv(step):
        here = half_group(row_far_peer, step, depth)
        return pltpu.make_async_remote_copy(
            here, here, send_px.at[step], recv_px.at[step], device_id=dev_p, device_id_type=MESH)

    def px_send_last(sub):
        here = last_piece(core, sub, depth)
        return remote(here, here, send_pl, recv_pl, sub, dev_p)

    def px_recv_last(sub):
        here = last_piece(1 - core, sub, depth)
        return remote(here, here, send_pl, recv_pl, sub, dev_p)

    def pz_send(num):
        here = piece(row_far, num, 1 - depth)
        return remote(here, here, send_pz, recv_pz, num, dev_p)

    def pz_recv(num):
        here = piece(row_far_peer, num, 1 - depth)
        return remote(here, here, send_pz, recv_pz, num, dev_p)

    def pz_send_last(num):
        here = last_piece(core, num, 1 - depth)
        return remote(here, here, send_pz, recv_pz, num, dev_p)

    def pz_recv_last(num):
        here = last_piece(1 - core, num, 1 - depth)
        return remote(here, here, send_pz, recv_pz, num, dev_p)

    def near_loads(step):
        slot = lax.rem(step, 2)
        pltpu.make_async_copy(
            b_ref.at[pl.ds(step * GROUP, GROUP), :],
            b_near.at[slot, pl.ds(core * GROUP, GROUP), :], load_near.at[slot]).start()
        pltpu.make_async_copy(
            ball.at[pl.ds(row_peer * band + step * GROUP, GROUP), :],
            b_near.at[slot, pl.ds((1 - core) * GROUP, GROUP), :], load_near.at[slot]).start()

    def near_wait(step):
        slot = lax.rem(step, 2)
        pltpu.make_async_copy(b_near.at[slot], b_near.at[slot], load_near.at[slot]).wait()

    def far_loads(step):
        slot = lax.rem(step, 2)
        pltpu.make_async_copy(
            ball.at[pl.ds(row_far * band + step * GROUP, GROUP), :],
            b_far.at[slot, pl.ds(core * GROUP, GROUP), :], load_far.at[slot]).start()
        pltpu.make_async_copy(
            ball.at[pl.ds(row_far_peer * band + step * GROUP, GROUP), :],
            b_far.at[slot, pl.ds((1 - core) * GROUP, GROUP), :], load_far.at[slot]).start()

    def far_wait(step):
        slot = lax.rem(step, 2)
        pltpu.make_async_copy(b_far.at[slot], b_far.at[slot], load_far.at[slot]).wait()

    def add(a_at, buf, slot, sub):
        at = pl.ds(pl.multiple_of(sub * TILE, TILE), TILE)
        acc[:, at] += jnp.dot(a_v[a_at], buf[slot, :, at], preferred_element_type=jnp.float32)

    def work(num):
        step = num // SUBS
        sub = lax.rem(num, SUBS)
        late = num - (FAR - 1)
        mul = num - FAR

        @pl.when(sub == 0)
        def _():
            own_recv(step).wait_recv()
            near_loads(step)

            @pl.when(step + 2 < steps)
            def _():
                own_send(step + 2).start()

            @pl.when(step >= 1)
            def _():
                a_recv(step - 1).wait_recv()
                near_wait(step - 1)

        @pl.when(step >= 1)
        def _():
            add(at_near + step - 1, b_near, lax.rem(step - 1, 2), sub)

        @pl.when((mul >= 0) & (lax.rem(mul + SUBS * 2, SUBS) == 0))
        def _():
            far_wait(mul // SUBS)

        @pl.when(mul >= 0)
        def _():
            add(at_far + mul // SUBS, b_far, lax.rem(mul // SUBS, 2), lax.rem(mul, SUBS))

        @pl.when((late >= 0) & (lax.rem(late + SUBS * 2, SUBS) == 0))
        def _():
            px_recv(late // SUBS).wait_recv()

            @pl.loop(0, SUBS)
            def _(k):
                pz_recv((late // SUBS) * SUBS + k).wait_recv()
            far_loads(late // SUBS)

    @pl.loop(0, steps)
    def _(step):
        a_load(step, 0).start()
        a_load(step, 1).start()

    barrier = pltpu.get_barrier_semaphore()
    for dev in (dev_x, dev_y, dev_z, dev_p):
        pl.semaphore_signal(barrier, inc=1, device_id=dev, device_id_type=MESH)
    pl.semaphore_wait(barrier, 4)

    @pl.loop(0, AHEAD)
    def _(num):
        x_send(num).start()

    own_send(0).start()
    own_send(1).start()

    @pl.loop(0, steps)
    def _(step):
        a_load_wait(step)
        a_send(step).start()

    @pl.loop(0, cols // TILE)
    def _(tile):
        at = pl.ds(pl.multiple_of(tile * TILE, TILE), TILE)
        acc[:, at] = jnp.zeros((rows_c, TILE), jnp.float32)

    body = count - SUBS

    @pl.loop(0, body)
    def _(num):
        x_recv(num).wait_recv()
        z_send(num).start()

        @pl.when(num + AHEAD < body)
        def _():
            x_send(num + AHEAD).start()

        @pl.when(num + AHEAD >= body)
        def _():
            @pl.when(num + AHEAD < count)
            def _():
                x_send_last(num + AHEAD).start()

            @pl.when((num + AHEAD >= count) & (num + AHEAD < count + SHIFT))
            def _():
                x_send_extra(num + AHEAD - SHIFT).start()

        @pl.when(lax.rem(num, SUBS) == SUBS - 1)
        def _():
            px_send(num // SUBS).start()

        @pl.when(num >= LAG)
        def _():
            z_recv(num - LAG).wait_recv()
            pz_send(num - LAG).start()

        work(num)

    @pl.loop(body, count)
    def _(num):
        x_recv_last(num).wait_recv()

        @pl.when(num < count - SHIFT)
        def _():
            z_send_last(num).start()
        px_send_last(num - body).start()

        @pl.when(num < body + LAG)
        def _():
            z_recv(num - LAG).wait_recv()
            pz_send(num - LAG).start()

        @pl.when(num >= body + LAG)
        def _():
            z_recv_last(num - LAG).wait_recv()
            pz_send_last(num - LAG).start()

        work(num)

    last = steps - 1

    def relay_out(num):
        z_recv_last(num).wait_recv()
        pz_send_last(num).start()

    def far_add(mul):
        add(at_far + last - 1, b_far, (last - 1) % 2, mul - (last - 1) * SUBS)

    for num in range(count - FAR, body):
        far_add(num)
        if num - (count - FAR) < LAG - 2:
            relay_out(count - LAG + num - (count - FAR))
    a_recv(last).wait_recv()
    near_wait(last)
    for sub in range(SUBS):
        add(at_near + last, b_near, last % 2, sub)
        if sub == SUBS // 2:
            relay_out(count - 2)
    relay_out(count - 1)

    def finish(at):
        total = acc[:, at] + jnp.dot(a_v[at_far + last], b_last[:, at], preferred_element_type=jnp.float32)
        o_v[:, at] = total.astype(o_v.dtype)

    per = TILE // width

    @pl.loop(0, half // TILE)
    def _(tile):
        for k in range(per):
            px_recv_last(tile * per + k).wait_recv()
        finish(pl.ds(pl.multiple_of(depth * half + tile * TILE, TILE), TILE))

    @pl.loop(0, half // TILE)
    def _(tile):
        for k in range(per):
            pz_recv_last(body + tile * per + k).wait_recv()
        finish(pl.ds(pl.multiple_of((1 - depth) * half + tile * TILE, TILE), TILE))

    @pl.loop(0, body)
    def _(num):
        x_send(num).wait_send()
        z_send(num).wait_send()
        pz_send(num).wait_send()

    @pl.loop(body, count)
    def _(num):
        x_send_last(num).wait_send()
        z_send_last(num).wait_send()
        pz_send_last(num).wait_send()
        px_send_last(num - body).wait_send()

    @pl.loop(0, steps)
    def _(step):
        a_send(step).wait_send()
        own_send(step).wait_send()

    @pl.loop(0, steps - 1)
    def _(step):
        px_send(step).wait_send()


def solution(mesh):
    def local_mm(a_blk, b_blk):
        band, cols = b_blk.shape
        rows_c = a_blk.shape[0] // 2
        steps = band // GROUP
        count = steps * SUBS
        any_spec = pl.BlockSpec(memory_space=pl.ANY)
        dma = pltpu.SemaphoreType.DMA
        c_blk, _ = pl.pallas_call(
            kernel,
            out_shape=(pltpu.VMEM((rows_c, cols), jnp.bfloat16),
                       jax.ShapeDtypeStruct((4 * band, cols), jnp.bfloat16)),
            in_specs=[any_spec] * 2,
            out_specs=(pl.BlockSpec(memory_space=pltpu.VMEM), any_spec),
            scratch_shapes=[
                pltpu.VMEM((2 * steps, rows_c, 2 * GROUP), jnp.bfloat16),
                pltpu.VMEM((rows_c, cols), jnp.float32),
                pltpu.VMEM((2, 2 * GROUP, cols), jnp.bfloat16),
                pltpu.VMEM((2, 2 * GROUP, cols), jnp.bfloat16),
                pltpu.VMEM((2 * GROUP, cols), jnp.bfloat16),
                dma((steps,)), dma((steps,)), dma((steps,)),
                dma((count,)), dma((count,)), dma((count,)), dma((count,)),
                dma((steps,)), dma((steps,)), dma((steps,)), dma((steps,)),
                dma((count,)), dma((count,)),
                dma((2,)), dma((2,)), dma((SUBS,)), dma((SUBS,)),
            ],
            compiler_params=pltpu.CompilerParams(
                collective_id=0, has_side_effects=True, vmem_limit_bytes=48 * 1024 * 1024),
            cost_estimate=pl.CostEstimate(
                flops=2 * rows_c * cols * 2 * cols, bytes_accessed=200 * 2 ** 20, transcendentals=0),
        )(a_blk, b_blk)
        return c_blk

    return jax.shard_map(
        local_mm, mesh=mesh, in_specs=(P("row", "col"), P("row", "col")),
        out_specs=P(("row", "depth"), "col"), check_vma=False)
```

time: 215 us -> 209 us (0.972)
  local copies, waits for them, and re-layouts: 7.89 us -> 3.4 us
    unnamed x1, local copies, waits for them, and re-layouts: 7.89 us -> 3.4 us
where the time goes in v2:
time: 209 us; the launch traced here: 208 us
  Pallas kernels  205 us (98%)
  local copies, waits for them, and re-layouts  3.4 us (2%)
    pallas_call x1, Pallas kernels, local_mm(): pl.pallas_call(kernel, out_shape=(pltpu.VMEM((rows_c, cols), jnp.bfloat16...  205 us

profile of v2, /device:TPU:0, one launch (start us, length us, event | category | flops | bytes accessed | tf_op | source)
XLA Modules:
  0.0 208.4 jit_solution(14803406818759599628)
XLA Ops:
  0.0 204.9 %shard_map.28 = (bf16[1024,4096]{1,0:T(8,128)(2,1)S(1)}, bf16[8192,4096]{1,0:T(8,128)(2,1)}) custom-call(bf16[2048,4096]{1,0:T(8,128)(2,1)} %a_ref.1, bf16[2048,4096]{1,0:T(8,128)(2,1)} %b_ref.1), custom_call_target="tpu_custom_call" | custom-call | flops 68719476736 | bytes 209715200 | tf_op jit(solution)/shard_map/pallas_call | solution.py:384
  205.0 3.4 %copy.4 = bf16[1024,4096]{1,0:T(8,128)(2,1)} copy(bf16[1024,4096]{1,0:T(8,128)(2,1)S(1)} %get-tuple-element.6) | data formatting | bytes 16777216

commit v3 on v0

v3 whole, which is shorter than its diff:
```python
import jax
import jax.numpy as jnp
from jax import lax
from jax.experimental import pallas as pl
from jax.experimental.pallas import tpu as pltpu
from jax.sharding import PartitionSpec as P

MESH = pl.DeviceIdType.MESH
GROUP = 128
SUBS = 8
AHEAD = 12
LAG = 4
SHIFT = 2
LOAD = 6
TILE = 512
WIDE = 1024


def kernel(a_ref, b_ref, o_v, ball, a_v, acc, b_v,
           load_a, send_a, recv_a, send_x, recv_x, send_z, recv_z, send_own, recv_own,
           send_px, recv_px, send_pz, recv_pz, load_far, load_near):
    depth = lax.axis_index("depth")
    col = lax.axis_index("col")
    row = lax.axis_index("row")
    core = lax.rem(row, 2)
    chip_x = row // 2
    rows_c = a_ref.shape[0] // 2
    band = b_ref.shape[0]
    cols = b_ref.shape[1]
    steps = band // GROUP
    last = steps - 1
    half = cols // 2
    width = half // SUBS
    count = steps * SUBS
    body = count - SUBS
    per = TILE // width
    tiles = half // TILE

    row_far = lax.rem(row + 2, 4)
    row_peer = chip_x * 2 + (1 - core)
    row_far_peer = lax.rem(row_peer + 2, 4)
    dev_x = (depth, col, row_far)
    dev_y = (depth, 1 - col, row)
    dev_z = (1 - depth, col, row)
    dev_p = (depth, col, row_peer)
    near = chip_x * 2 * GROUP
    far = (1 - chip_x) * 2 * GROUP

    def slot_of(step):
        return lax.rem(step, 2)

    def remote(src, dst, send, recv, num, dev):
        return pltpu.make_async_remote_copy(
            src, dst, send.at[num], recv.at[num], device_id=dev, device_id_type=MESH)

    def a_cols(step, side):
        return a_v.at[step, :, pl.ds(side * 2 * GROUP, 2 * GROUP)]

    def a_load(step, part):
        return pltpu.make_async_copy(
            a_ref.at[pl.ds(depth * rows_c, rows_c), pl.ds(part * band + step * GROUP, GROUP)],
            a_v.at[step, :, pl.ds(col * 2 * GROUP + part * GROUP, GROUP)], load_a.at[step])

    def a_load_wait(step):
        pltpu.make_async_copy(a_cols(step, col), a_cols(step, col), load_a.at[step]).wait()

    def a_send(step):
        return remote(a_cols(step, col), a_cols(step, col), send_a, recv_a, step, dev_y)

    def a_recv(step):
        return remote(a_cols(step, 1 - col), a_cols(step, 1 - col), send_a, recv_a, step, dev_y)

    def piece(band_row, num, which):
        return ball.at[pl.ds(band_row * band + (num // SUBS) * GROUP, GROUP),
                       pl.ds(which * half + lax.rem(num, SUBS) * width, width)]

    def last_piece(core_of, num, which, first=far):
        return b_v.at[2, pl.ds(first + core_of * GROUP, GROUP),
                      pl.ds(which * half + lax.rem(num, SUBS) * width, width)]

    def source(num, which):
        return b_ref.at[pl.ds((num // SUBS) * GROUP, GROUP),
                        pl.ds(which * half + lax.rem(num, SUBS) * width, width)]

    def mine(num, which, is_last):
        return last_piece(core, num, which) if is_last else piece(row_far, num, which)

    def peers(num, which, is_last):
        return last_piece(1 - core, num, which) if is_last else piece(row_far_peer, num, which)

    def x_send(num, is_last):
        dst = last_piece(core, num, depth, near) if is_last else piece(row, num, depth)
        return remote(source(num, depth), dst, send_x, recv_x, num, dev_x)

    def x_send_extra(num):
        return remote(source(num, 1 - depth), last_piece(core, num, 1 - depth, near), send_z, recv_z, num, dev_x)

    def x_recv(num, is_last):
        here = mine(num, depth, is_last)
        return remote(here, here, send_x, recv_x, num, dev_x)

    def z_send(num, is_last):
        here = mine(num, depth, is_last)
        return remote(here, here, send_z, recv_z, num, dev_z)

    def z_recv(num, is_last):
        here = mine(num, 1 - depth, is_last)
        return remote(here, here, send_z, recv_z, num, dev_z)

    def px_send(num, is_last):
        here = mine(num, depth, is_last)
        return remote(here, here, send_px, recv_px, num, dev_p)

    def px_recv(num, is_last):
        here = peers(num, depth, is_last)
        return remote(here, here, send_px, recv_px, num, dev_p)

    def pz_send(num, is_last):
        here = mine(num, 1 - depth, is_last)
        return remote(here, here, send_pz, recv_pz, num, dev_p)

    def pz_recv(num, is_last):
        here = peers(num, 1 - depth, is_last)
        return remote(here, here, send_pz, recv_pz, num, dev_p)

    def own_send(step):
        return remote(
            b_ref.at[pl.ds(step * GROUP, GROUP), :], ball.at[pl.ds(row * band + step * GROUP, GROUP), :],
            send_own, recv_own, step, dev_p)

    def own_recv(step):
        here = ball.at[pl.ds(row_peer * band + step * GROUP, GROUP), :]
        return remote(here, here, send_own, recv_own, step, dev_p)

    def near_loads(step, slot):
        pltpu.make_async_copy(
            b_ref.at[pl.ds(step * GROUP, GROUP), :],
            b_v.at[slot, pl.ds(near + core * GROUP, GROUP), :], load_near.at[lax.rem(step, 2)]).start()
        pltpu.make_async_copy(
            ball.at[pl.ds(row_peer * band + step * GROUP, GROUP), :],
            b_v.at[slot, pl.ds(near + (1 - core) * GROUP, GROUP), :], load_near.at[lax.rem(step, 2)]).start()

    def near_wait(step, slot):
        here = b_v.at[slot, pl.ds(near, 2 * GROUP), :]
        pltpu.make_async_copy(here, here, load_near.at[lax.rem(step, 2)]).wait()

    def tile_cols(num):
        at = lax.rem(num, 2 * tiles)
        which = jnp.where(at < tiles, depth, 1 - depth)
        return pl.ds(pl.multiple_of(which * half + lax.rem(at, tiles) * TILE, TILE), TILE)

    def far_loads(num):
        step = num // SUBS
        slot = slot_of(step)
        at = tile_cols(num)
        for band_row, part in ((row_far, core), (row_far_peer, 1 - core)):
            pltpu.make_async_copy(
                ball.at[pl.ds(band_row * band + step * GROUP, GROUP), at],
                b_v.at[slot, pl.ds(far + part * GROUP, GROUP), at], load_far.at[lax.rem(num, SUBS)]).start()

    def far_wait(num):
        here = b_v.at[slot_of(num // SUBS), pl.ds(far, 2 * GROUP), tile_cols(num)]
        pltpu.make_async_copy(here, here, load_far.at[lax.rem(num, SUBS)]).wait()

    def work(num, to_load):
        step = num // SUBS
        sub = lax.rem(num, SUBS)

        @pl.when(sub == 0)
        def _():
            own_recv(step).wait_recv()
            if to_load:
                near_loads(step, slot_of(step))

                @pl.when(step + 2 < steps)
                def _():
                    own_send(step + 2).start()
            else:
                near_loads(step, 2)

            @pl.when(step >= 1)
            def _():
                a_recv(step - 1).wait_recv()
                near_wait(step - 1, slot_of(step - 1))

        @pl.when((num >= LOAD) & (num < body + LOAD))
        def _():
            new = num - LOAD
            at = lax.rem(new, 2 * tiles)
            first = (new // SUBS) * SUBS + lax.rem(at, tiles) * per

            @pl.when(at < tiles)
            def _():
                for k in range(per):
                    px_recv(first + k, False).wait_recv()

            @pl.when(at >= tiles)
            def _():
                for k in range(per):
                    pz_recv(first + k, False).wait_recv()
            far_loads(new)

        @pl.when(step >= 1)
        def _():
            far_wait(num - SUBS)
            at = tile_cols(num)
            acc[:, at] += jnp.dot(a_v[step - 1], b_v[slot_of(step - 1), :, at], preferred_element_type=jnp.float32)

    @pl.loop(0, steps)
    def _(step):
        a_load(step, 0).start()
        a_load(step, 1).start()

    barrier = pltpu.get_barrier_semaphore()
    for dev in (dev_x, dev_y, dev_z, dev_p):
        pl.semaphore_signal(barrier, inc=1, device_id=dev, device_id_type=MESH)
    pl.semaphore_wait(barrier, 4)

    @pl.loop(0, AHEAD)
    def _(num):
        x_send(num, False).start()

    own_send(0).start()
    own_send(1).start()

    @pl.loop(0, steps)
    def _(step):
        a_load_wait(step)
        a_send(step).start()

    @pl.loop(0, cols // TILE)
    def _(tile):
        at = pl.ds(pl.multiple_of(tile * TILE, TILE), TILE)
        acc[:, at] = jnp.zeros((rows_c, TILE), jnp.float32)

    @pl.loop(0, body)
    def _(num):
        x_recv(num, False).wait_recv()
        z_send(num, False).start()
        px_send(num, False).start()

        @pl.when(num + AHEAD < body)
        def _():
            x_send(num + AHEAD, False).start()

        @pl.when((num + AHEAD >= body) & (num + AHEAD < count))
        def _():
            x_send(num + AHEAD, True).start()

        @pl.when((num + AHEAD >= count) & (num + AHEAD < count + SHIFT))
        def _():
            x_send_extra(num + AHEAD - SHIFT).start()

        @pl.when(num >= LAG)
        def _():
            z_recv(num - LAG, False).wait_recv()
            pz_send(num - LAG, False).start()

        work(num, True)

    @pl.loop(body, count)
    def _(num):
        x_recv(num, True).wait_recv()

        @pl.when(num < count - SHIFT)
        def _():
            z_send(num, True).start()
        px_send(num, True).start()

        @pl.when(num < body + LAG)
        def _():
            z_recv(num - LAG, False).wait_recv()
            pz_send(num - LAG, False).start()

        @pl.when(num >= body + LAG)
        def _():
            z_recv(num - LAG, True).wait_recv()
            pz_send(num - LAG, True).start()

        work(num, False)

    def relay_out(num):
        z_recv(num, True).wait_recv()
        pz_send(num, True).start()

    relay_out(count - 4)
    a_recv(last).wait_recv()
    near_wait(last, 2)
    wide = half // WIDE
    for part in range(2 * wide):
        which = depth if part < wide else 1 - depth
        first = (part % wide) * (WIDE // width)
        for k in range(WIDE // width):
            if part < wide:
                px_recv(body + first + k, True).wait_recv()
            else:
                pz_recv(body + first + k, True).wait_recv()
        at = pl.ds(pl.multiple_of(which * half + (part % wide) * WIDE, WIDE), WIDE)
        total = acc[:, at] + jnp.dot(a_v[last], b_v[2, :, at], preferred_element_type=jnp.float32)
        o_v[:, at] = total.astype(o_v.dtype)
        if part < 3:
            relay_out(count - 3 + part)

    @pl.loop(0, body)
    def _(num):
        x_send(num, False).wait_send()
        z_send(num, False).wait_send()
        px_send(num, False).wait_send()
        pz_send(num, False).wait_send()

    @pl.loop(body, count)
    def _(num):
        x_send(num, True).wait_send()
        z_send(num, True).wait_send()
        px_send(num, True).wait_send()
        pz_send(num, True).wait_send()

    @pl.loop(0, steps)
    def _(step):
        a_send(step).wait_send()
        own_send(step).wait_send()


def solution(mesh):
    def local_mm(a_blk, b_blk):
        band, cols = b_blk.shape
        rows_c = a_blk.shape[0] // 2
        steps = band // GROUP
        count = steps * SUBS
        any_spec = pl.BlockSpec(memory_space=pl.ANY)
        dma = pltpu.SemaphoreType.DMA
        c_blk, _ = pl.pallas_call(
            kernel,
            out_shape=(pltpu.VMEM((rows_c, cols), jnp.bfloat16),
                       jax.ShapeDtypeStruct((4 * band, cols), jnp.bfloat16)),
            in_specs=[any_spec] * 2,
            out_specs=(pl.BlockSpec(memory_space=pltpu.VMEM), any_spec),
            scratch_shapes=[
                pltpu.VMEM((steps, rows_c, 4 * GROUP), jnp.bfloat16),
                pltpu.VMEM((rows_c, cols), jnp.float32),
                pltpu.VMEM((3, 4 * GROUP, cols), jnp.bfloat16),
                dma((steps,)), dma((steps,)), dma((steps,)),
                dma((count,)), dma((count,)), dma((count,)), dma((count,)),
                dma((steps,)), dma((steps,)),
                dma((count,)), dma((count,)), dma((count,)), dma((count,)),
                dma((SUBS,)), dma((2,)),
            ],
            compiler_params=pltpu.CompilerParams(
                collective_id=0, has_side_effects=True, vmem_limit_bytes=52 * 1024 * 1024),
            cost_estimate=pl.CostEstimate(
                flops=2 * rows_c * cols * 2 * cols, bytes_accessed=200 * 2 ** 20, transcendentals=0),
        )(a_blk, b_blk)
        return c_blk

    return jax.shard_map(
        local_mm, mesh=mesh, in_specs=(P("row", "col"), P("row", "col")),
        out_specs=P(("row", "depth"), "col"), check_vma=False)
```

time: 1130 us -> 207 us (0.18); the launches traced: 1120 us -> 207 us
  waiting for transfers between devices: 728 us -> 0 us
  starting transfers between devices: 259 us -> 0 us
  Pallas kernels: 0 us -> 203 us
  matrix products: 89.6 us -> 0 us
  other arithmetic: 25.6 us -> 0 us
  between operations: 13.4 us -> 0.01 us
    reduce_scatter x1 -> x0, waiting for transfers between devices: 495 us -> none  [local_mm(): lax.psum_scatter(part_sum, 'depth', scatter_dimension=0, tiled=True)]
    ppermute x4 -> x0, starting transfers between devices: 259 us -> none  [the longest x1 127 us: local_mm(): a_first = lax.ppermute(a_blk, AXES_ALL, pairs_a0)]
    ppermute x4 -> x0, waiting for transfers between devices: 233 us -> none  [the longest x1 233 us: local_mm(): a_second = lax.ppermute(a_blk, AXES_ALL, pairs_a1)]
    pallas_call x0 -> x1, Pallas kernels: none -> 203 us  [local_mm(): pl.pallas_call(kernel, out_shape=(pltpu.VMEM((rows_c, cols), jnp.bfloat16...]
    dot_general x2 -> x0, matrix products: 89.6 us -> none  [local_mm(): block_prod = jnp.dot(a_cur, b_cur, preferred_element_type=jnp.float32)]
    concatenate x1 -> x0, other arithmetic: 16.6 us -> none  [local_mm(): a_joined = jnp.concatenate([a_first, a_second], axis=1)]
  transfers between devices with their start and end apart: 5 -> 0, of which waited for: 2 -> 0; matrix products, arithmetic and copies ran while one was open for 5% -> 0% of each run, Pallas kernels for 0% -> 0%
where the time goes in v3:
time: 207 us
  Pallas kernels  203 us (98%)
  local copies, waits for them, and re-layouts  3.4 us (2%)
    pallas_call x1, Pallas kernels, local_mm(): pl.pallas_call(kernel, out_shape=(pltpu.VMEM((rows_c, cols), jnp.bfloat16...  203 us

profile of v3, /device:TPU:0, one launch (start us, length us, event | category | flops | bytes accessed | tf_op | source)
XLA Modules:
  0.0 206.9 jit_solution(3619291810078249894)
XLA Ops:
  0.0 203.4 %shard_map.28 = (bf16[1024,4096]{1,0:T(8,128)(2,1)S(1)}, bf16[8192,4096]{1,0:T(8,128)(2,1)}) custom-call(bf16[2048,4096]{1,0:T(8,128)(2,1)} %a_ref.1, bf16[2048,4096]{1,0:T(8,128)(2,1)} %b_ref.1), custom_call_target="tpu_custom_call" | custom-call | flops 68719476736 | bytes 209715200 | tf_op jit(solution)/shard_map/pallas_call | solution.py:332
  203.5 3.4 %copy.4 = bf16[1024,4096]{1,0:T(8,128)(2,1)} copy(bf16[1024,4096]{1,0:T(8,128)(2,1)S(1)} %get-tuple-element.6) | data formatting | bytes 16777216

commit v4 on v3

--- a/solution.py
+++ b/solution.py
@@ -8,9 +8,9 @@
 MESH = pl.DeviceIdType.MESH
 GROUP = 128
 SUBS = 8
-AHEAD = 12
+AHEAD = 16
 LAG = 4
-SHIFT = 2
+SHIFT = 6
 LOAD = 6
 TILE = 512
 WIDE = 1024

time: 207 us -> 211 us (1.019)
  Pallas kernels: 203 us -> 207 us
    pallas_call x1, Pallas kernels: 203 us -> 207 us  [local_mm(): pl.pallas_call(kernel, out_shape=(pltpu.VMEM((rows_c, cols), jnp.bfloat16...]
where the time goes in v4:
time: 211 us; the launch traced here: 210 us
  Pallas kernels  207 us (98%)
  local copies, waits for them, and re-layouts  3.4 us (2%)
    pallas_call x1, Pallas kernels, local_mm(): pl.pallas_call(kernel, out_shape=(pltpu.VMEM((rows_c, cols), jnp.bfloat16...  207 us

profile of v4, /device:TPU:0, one launch (start us, length us, event | category | flops | bytes accessed | tf_op | source)
XLA Modules:
  0.0 210.5 jit_solution(15967429524427711719)
XLA Ops:
  0.0 207.1 %shard_map.28 = (bf16[1024,4096]{1,0:T(8,128)(2,1)S(1)}, bf16[8192,4096]{1,0:T(8,128)(2,1)}) custom-call(bf16[2048,4096]{1,0:T(8,128)(2,1)} %a_ref.1, bf16[2048,4096]{1,0:T(8,128)(2,1)} %b_ref.1), custom_call_target="tpu_custom_call" | custom-call | flops 68719476736 | bytes 209715200 | tf_op jit(solution)/shard_map/pallas_call | solution.py:332
  207.1 3.4 %copy.4 = bf16[1024,4096]{1,0:T(8,128)(2,1)} copy(bf16[1024,4096]{1,0:T(8,128)(2,1)S(1)} %get-tuple-element.6) | data formatting | bytes 16777216

commit v5 on v3

--- a/solution.py
+++ b/solution.py
@@ -216,7 +216,17 @@
         pl.semaphore_signal(barrier, inc=1, device_id=dev, device_id_type=MESH)
     pl.semaphore_wait(barrier, 4)
 
-    @pl.loop(0, AHEAD)
+    @pl.when(core == 0)
+    def _():
+        x_send(0, False).start()
+
+    @pl.when(core == 1)
+    def _():
+        for k in range(2):
+            rows = pl.ds(k * GROUP // 2, GROUP // 2)
+            remote(source(0, depth).at[rows], piece(row, 0, depth).at[rows], send_x, recv_x, 0, dev_x).start()
+
+    @pl.loop(1, AHEAD)
     def _(num):
         x_send(num, False).start()
 

time: 207 us -> 207 us (level)
  no operation moved by 1% of the time
where the time goes in v5:
time: 207 us
  Pallas kernels  203 us (98%)
  local copies, waits for them, and re-layouts  3.4 us (2%)
    pallas_call x1, Pallas kernels, local_mm(): pl.pallas_call(kernel, out_shape=(pltpu.VMEM((rows_c, cols), jnp.bfloat16...  203 us

profile of v5, /device:TPU:0, one launch (start us, length us, event | category | flops | bytes accessed | tf_op | source)
XLA Modules:
  0.0 206.9 jit_solution(4044594039389537618)
XLA Ops:
  0.0 203.4 %shard_map.28 = (bf16[1024,4096]{1,0:T(8,128)(2,1)S(1)}, bf16[8192,4096]{1,0:T(8,128)(2,1)}) custom-call(bf16[2048,4096]{1,0:T(8,128)(2,1)} %a_ref.1, bf16[2048,4096]{1,0:T(8,128)(2,1)} %b_ref.1), custom_call_target="tpu_custom_call" | custom-call | flops 68719476736 | bytes 209715200 | tf_op jit(solution)/shard_map/pallas_call | solution.py:342
  203.5 3.4 %copy.4 = bf16[1024,4096]{1,0:T(8,128)(2,1)} copy(bf16[1024,4096]{1,0:T(8,128)(2,1)S(1)} %get-tuple-element.6) | data formatting | bytes 16777216

commit v6 on v4

--- a/solution.py
+++ b/solution.py
@@ -7,12 +7,12 @@
 
 MESH = pl.DeviceIdType.MESH
 GROUP = 128
-SUBS = 8
-AHEAD = 16
-LAG = 4
-SHIFT = 6
-LOAD = 6
-TILE = 512
+SUBS = 4
+AHEAD = 6
+LAG = 2
+SHIFT = 1
+LOAD = 3
+TILE = 1024
 WIDE = 1024
 
 
@@ -283,7 +283,8 @@
         z_recv(num, True).wait_recv()
         pz_send(num, True).start()
 
-    relay_out(count - 4)
+    for num in range(count - LAG, count - 1):
+        relay_out(num)
     a_recv(last).wait_recv()
     near_wait(last, 2)
     wide = half // WIDE
@@ -298,8 +299,8 @@
         at = pl.ds(pl.multiple_of(which * half + (part % wide) * WIDE, WIDE), WIDE)
         total = acc[:, at] + jnp.dot(a_v[last], b_v[2, :, at], preferred_element_type=jnp.float32)
         o_v[:, at] = total.astype(o_v.dtype)
-        if part < 3:
-            relay_out(count - 3 + part)
+        if part == 1:
+            relay_out(count - 1)
 
     @pl.loop(0, body)
     def _(num):

time: 211 us -> 203 us (0.962)
  Pallas kernels: 207 us -> 199 us
    pallas_call x1, Pallas kernels: 207 us -> 199 us  [local_mm(): pl.pallas_call(kernel, out_shape=(pltpu.VMEM((rows_c, cols), jnp.bfloat16...]
where the time goes in v6:
time: 203 us; the launch traced here: 202 us
  Pallas kernels  199 us (98%)
  local copies, waits for them, and re-layouts  3.4 us (2%)
    pallas_call x1, Pallas kernels, local_mm(): pl.pallas_call(kernel, out_shape=(pltpu.VMEM((rows_c, cols), jnp.bfloat16...  199 us

profile of v6, /device:TPU:0, one launch (start us, length us, event | category | flops | bytes accessed | tf_op | source)
XLA Modules:
  0.0 202.5 jit_solution(12376002338348779776)
XLA Ops:
  0.0 199.1 %shard_map.28 = (bf16[1024,4096]{1,0:T(8,128)(2,1)S(1)}, bf16[8192,4096]{1,0:T(8,128)(2,1)}) custom-call(bf16[2048,4096]{1,0:T(8,128)(2,1)} %a_ref.1, bf16[2048,4096]{1,0:T(8,128)(2,1)} %b_ref.1), custom_call_target="tpu_custom_call" | custom-call | flops 68719476736 | bytes 209715200 | tf_op jit(solution)/shard_map/pallas_call | solution.py:333
  199.1 3.4 %copy.4 = bf16[1024,4096]{1,0:T(8,128)(2,1)} copy(bf16[1024,4096]{1,0:T(8,128)(2,1)S(1)} %get-tuple-element.6) | data formatting | bytes 16777216

commit v7 on v6

--- a/solution.py
+++ b/solution.py
@@ -13,6 +13,7 @@
 SHIFT = 1
 LOAD = 3
 TILE = 1024
+BACK = 8
 WIDE = 1024
 
 
@@ -162,6 +163,12 @@
         here = b_v.at[slot_of(num // SUBS), pl.ds(far, 2 * GROUP), tile_cols(num)]
         pltpu.make_async_copy(here, here, load_far.at[lax.rem(num, SUBS)]).wait()
 
+    def sent(num, is_last):
+        x_send(num, is_last).wait_send()
+        z_send(num, is_last).wait_send()
+        px_send(num, is_last).wait_send()
+        pz_send(num, is_last).wait_send()
+
     def work(num, to_load):
         step = num // SUBS
         sub = lax.rem(num, SUBS)
@@ -178,6 +185,11 @@
             else:
                 near_loads(step, 2)
 
+            @pl.when(step >= 2)
+            def _():
+                a_send(step - 2).wait_send()
+                own_send(step - 2).wait_send()
+
             @pl.when(step >= 1)
             def _():
                 a_recv(step - 1).wait_recv()
@@ -206,14 +218,19 @@
             at = tile_cols(num)
             acc[:, at] += jnp.dot(a_v[step - 1], b_v[slot_of(step - 1), :, at], preferred_element_type=jnp.float32)
 
+        @pl.when(num >= BACK)
+        def _():
+            sent(num - BACK, False)
+
+    barrier = pltpu.get_barrier_semaphore()
+    for dev in (dev_x, dev_y, dev_z, dev_p):
+        pl.semaphore_signal(barrier, inc=1, device_id=dev, device_id_type=MESH)
+
     @pl.loop(0, steps)
     def _(step):
         a_load(step, 0).start()
         a_load(step, 1).start()
 
-    barrier = pltpu.get_barrier_semaphore()
-    for dev in (dev_x, dev_y, dev_z, dev_p):
-        pl.semaphore_signal(barrier, inc=1, device_id=dev, device_id_type=MESH)
     pl.semaphore_wait(barrier, 4)
 
     @pl.loop(0, AHEAD)
@@ -302,21 +319,15 @@
         if part == 1:
             relay_out(count - 1)
 
-    @pl.loop(0, body)
-    def _(num):
-        x_send(num, False).wait_send()
-        z_send(num, False).wait_send()
-        px_send(num, False).wait_send()
-        pz_send(num, False).wait_send()
+    @pl.loop(count - BACK, body)
+    def _(num):
+        sent(num, False)
 
     @pl.loop(body, count)
     def _(num):
-        x_send(num, True).wait_send()
-        z_send(num, True).wait_send()
-        px_send(num, True).wait_send()
-        pz_send(num, True).wait_send()
-
-    @pl.loop(0, steps)
+        sent(num, True)
+
+    @pl.loop(steps - 2, steps)
     def _(step):
         a_send(step).wait_send()
         own_send(step).wait_send()

time: 203 us -> 202 us (level)
  no operation moved by 1% of the time
where the time goes in v7:
time: 202 us
  Pallas kernels  198 us (98%)
  local copies, waits for them, and re-layouts  3.4 us (2%)
    pallas_call x1, Pallas kernels, local_mm(): pl.pallas_call(kernel, out_shape=(pltpu.VMEM((rows_c, cols), jnp.bfloat16...  198 us

profile of v7, /device:TPU:0, one launch (start us, length us, event | category | flops | bytes accessed | tf_op | source)
XLA Modules:
  0.0 201.7 jit_solution(2462641152120450533)
XLA Ops:
  0.0 198.3 %shard_map.28 = (bf16[1024,4096]{1,0:T(8,128)(2,1)S(1)}, bf16[8192,4096]{1,0:T(8,128)(2,1)}) custom-call(bf16[2048,4096]{1,0:T(8,128)(2,1)} %a_ref.1, bf16[2048,4096]{1,0:T(8,128)(2,1)} %b_ref.1), custom_call_target="tpu_custom_call" | custom-call | flops 68719476736 | bytes 209715200 | tf_op jit(solution)/shard_map/pallas_call | solution.py:344
  198.3 3.4 %copy.4 = bf16[1024,4096]{1,0:T(8,128)(2,1)} copy(bf16[1024,4096]{1,0:T(8,128)(2,1)S(1)} %get-tuple-element.6) | data formatting | bytes 16777216

commit v8 on v7

--- a/solution.py
+++ b/solution.py
@@ -169,31 +169,31 @@
         px_send(num, is_last).wait_send()
         pz_send(num, is_last).wait_send()
 
-    def work(num, to_load):
+    def multiply(num, slot):
         step = num // SUBS
-        sub = lax.rem(num, SUBS)
-
-        @pl.when(sub == 0)
+
+        @pl.when(lax.rem(num, SUBS) == 0)
         def _():
             own_recv(step).wait_recv()
-            if to_load:
-                near_loads(step, slot_of(step))
-
-                @pl.when(step + 2 < steps)
-                def _():
-                    own_send(step + 2).start()
-            else:
-                near_loads(step, 2)
-
-            @pl.when(step >= 2)
+            near_loads(step, slot)
+
+            @pl.when(step + 2 < steps)
             def _():
-                a_send(step - 2).wait_send()
-                own_send(step - 2).wait_send()
+                own_send(step + 2).start()
 
             @pl.when(step >= 1)
             def _():
                 a_recv(step - 1).wait_recv()
                 near_wait(step - 1, slot_of(step - 1))
+
+        @pl.when(step >= 1)
+        def _():
+            far_wait(num - SUBS)
+            at = tile_cols(num)
+            acc[:, at] += jnp.dot(a_v[step - 1], b_v[slot_of(step - 1), :, at], preferred_element_type=jnp.float32)
+
+    def load(num):
+        step = num // SUBS
 
         @pl.when((num >= LOAD) & (num < body + LOAD))
         def _():
@@ -212,15 +212,14 @@
                     pz_recv(first + k, False).wait_recv()
             far_loads(new)
 
-        @pl.when(step >= 1)
-        def _():
-            far_wait(num - SUBS)
-            at = tile_cols(num)
-            acc[:, at] += jnp.dot(a_v[step - 1], b_v[slot_of(step - 1), :, at], preferred_element_type=jnp.float32)
-
         @pl.when(num >= BACK)
         def _():
             sent(num - BACK, False)
+
+        @pl.when((lax.rem(num, SUBS) == 0) & (step >= 2))
+        def _():
+            a_send(step - 2).wait_send()
+            own_send(step - 2).wait_send()
 
     barrier = pltpu.get_barrier_semaphore()
     for dev in (dev_x, dev_y, dev_z, dev_p):
@@ -233,14 +232,18 @@
 
     pl.semaphore_wait(barrier, 4)
 
-    @pl.loop(0, AHEAD)
+    x_send(0, False).start()
+    a_load_wait(0)
+    a_send(0).start()
+
+    @pl.loop(1, AHEAD)
     def _(num):
         x_send(num, False).start()
 
     own_send(0).start()
     own_send(1).start()
 
-    @pl.loop(0, steps)
+    @pl.loop(1, steps)
     def _(step):
         a_load_wait(step)
         a_send(step).start()
@@ -268,12 +271,14 @@
         def _():
             x_send_extra(num + AHEAD - SHIFT).start()
 
+        multiply(num, slot_of(num // SUBS))
+
         @pl.when(num >= LAG)
         def _():
             z_recv(num - LAG, False).wait_recv()
             pz_send(num - LAG, False).start()
 
-        work(num, True)
+        load(num)
 
     @pl.loop(body, count)
     def _(num):
@@ -283,6 +288,7 @@
         def _():
             z_send(num, True).start()
         px_send(num, True).start()
+        multiply(num, 2)
 
         @pl.when(num < body + LAG)
         def _():
@@ -294,14 +300,12 @@
             z_recv(num - LAG, True).wait_recv()
             pz_send(num - LAG, True).start()
 
-        work(num, False)
+        load(num)
 
     def relay_out(num):
         z_recv(num, True).wait_recv()
         pz_send(num, True).start()
 
-    for num in range(count - LAG, count - 1):
-        relay_out(num)
     a_recv(last).wait_recv()
     near_wait(last, 2)
     wide = half // WIDE
@@ -316,8 +320,8 @@
         at = pl.ds(pl.multiple_of(which * half + (part % wide) * WIDE, WIDE), WIDE)
         total = acc[:, at] + jnp.dot(a_v[last], b_v[2, :, at], preferred_element_type=jnp.float32)
         o_v[:, at] = total.astype(o_v.dtype)
-        if part == 1:
-            relay_out(count - 1)
+        if part < LAG:
+            relay_out(count - LAG + part)
 
     @pl.loop(count - BACK, body)
     def _(num):

time: 202 us -> 202 us (level)
  no operation moved by 1% of the time
where the time goes in v8:
time: 202 us; the launch traced here: 201 us
  Pallas kernels  198 us (98%)
  local copies, waits for them, and re-layouts  3.4 us (2%)
    pallas_call x1, Pallas kernels, local_mm(): pl.pallas_call(kernel, out_shape=(pltpu.VMEM((rows_c, cols), jnp.bfloat16...  198 us

profile of v8, /device:TPU:0, one launch (start us, length us, event | category | flops | bytes accessed | tf_op | source)
XLA Modules:
  0.0 201.3 jit_solution(4078995181019598875)
XLA Ops:
  0.0 197.9 %shard_map.28 = (bf16[1024,4096]{1,0:T(8,128)(2,1)S(1)}, bf16[8192,4096]{1,0:T(8,128)(2,1)}) custom-call(bf16[2048,4096]{1,0:T(8,128)(2,1)} %a_ref.1, bf16[2048,4096]{1,0:T(8,128)(2,1)} %b_ref.1), custom_call_target="tpu_custom_call" | custom-call | flops 68719476736 | bytes 209715200 | tf_op jit(solution)/shard_map/pallas_call | solution.py:348
  197.9 3.4 %copy.4 = bf16[1024,4096]{1,0:T(8,128)(2,1)} copy(bf16[1024,4096]{1,0:T(8,128)(2,1)S(1)} %get-tuple-element.6) | data formatting | bytes 16777216

commit v9 on v8

v9 whole, which is shorter than its diff:
```python
import jax
import jax.numpy as jnp
from jax import lax
from jax.experimental import pallas as pl
from jax.experimental.pallas import tpu as pltpu
from jax.sharding import PartitionSpec as P

MESH = pl.DeviceIdType.MESH
GROUP = 128
SUBS = 4
AHEAD = 6
LAG = 2
FINE = 8
FINE_LAG = 4
SHIFT = 2
LOAD = 3
TILE = 1024
BACK = 8
HALF_TILE = 512
LOADS = (0, 2, 5)


def kernel(a_ref, b_ref, o_v, ball, a_v, acc, b_v,
           load_a, send_a, recv_a, send_x, recv_x, send_z, recv_z, send_own, recv_own,
           send_px, recv_px, send_pz, recv_pz, load_far, load_near,
           send_xl, recv_xl, send_zl, recv_zl, send_pxl, recv_pxl, send_pzl, recv_pzl):
    depth = lax.axis_index("depth")
    col = lax.axis_index("col")
    row = lax.axis_index("row")
    core = lax.rem(row, 2)
    chip_x = row // 2
    rows_c = a_ref.shape[0] // 2
    band = b_ref.shape[0]
    cols = b_ref.shape[1]
    steps = band // GROUP
    last = steps - 1
    half = cols // 2
    width = half // SUBS
    fine = half // FINE
    body = last * SUBS
    per = TILE // width
    tiles = half // TILE

    row_far = lax.rem(row + 2, 4)
    row_peer = chip_x * 2 + (1 - core)
    row_far_peer = lax.rem(row_peer + 2, 4)
    dev_x = (depth, col, row_far)
    dev_y = (depth, 1 - col, row)
    dev_z = (1 - depth, col, row)
    dev_p = (depth, col, row_peer)
    near = chip_x * 2 * GROUP
    far = (1 - chip_x) * 2 * GROUP

    def slot_of(step):
        return lax.rem(step, 2)

    def remote(src, dst, send, recv, num, dev):
        return pltpu.make_async_remote_copy(
            src, dst, send.at[num], recv.at[num], device_id=dev, device_id_type=MESH)

    def a_cols(step, side):
        return a_v.at[step, :, pl.ds(side * 2 * GROUP, 2 * GROUP)]

    def a_load(step, part):
        return pltpu.make_async_copy(
            a_ref.at[pl.ds(depth * rows_c, rows_c), pl.ds(part * band + step * GROUP, GROUP)],
            a_v.at[step, :, pl.ds(col * 2 * GROUP + part * GROUP, GROUP)], load_a.at[step])

    def a_load_wait(step):
        pltpu.make_async_copy(a_cols(step, col), a_cols(step, col), load_a.at[step]).wait()

    def a_send(step):
        return remote(a_cols(step, col), a_cols(step, col), send_a, recv_a, step, dev_y)

    def a_recv(step):
        return remote(a_cols(step, 1 - col), a_cols(step, 1 - col), send_a, recv_a, step, dev_y)

    def piece(band_row, num, which):
        return ball.at[pl.ds(band_row * band + (num // SUBS) * GROUP, GROUP),
                       pl.ds(which * half + lax.rem(num, SUBS) * width, width)]

    def source(num, which):
        return b_ref.at[pl.ds((num // SUBS) * GROUP, GROUP),
                        pl.ds(which * half + lax.rem(num, SUBS) * width, width)]

    def x_send(num):
        return remote(source(num, depth), piece(row, num, depth), send_x, recv_x, num, dev_x)

    def x_recv(num):
        here = piece(row_far, num, depth)
        return remote(here, here, send_x, recv_x, num, dev_x)

    def z_send(num):
        here = piece(row_far, num, depth)
        return remote(here, here, send_z, recv_z, num, dev_z)

    def z_recv(num):
        here = piece(row_far, num, 1 - depth)
        return remote(here, here, send_z, recv_z, num, dev_z)

    def px_send(num):
        here = piece(row_far, num, depth)
        return remote(here, here, send_px, recv_px, num, dev_p)

    def px_recv(num):
        here = piece(row_far_peer, num, depth)
        return remote(here, here, send_px, recv_px, num, dev_p)

    def pz_send(num):
        here = piece(row_far, num, 1 - depth)
        return remote(here, here, send_pz, recv_pz, num, dev_p)

    def pz_recv(num):
        here = piece(row_far_peer, num, 1 - depth)
        return remote(here, here, send_pz, recv_pz, num, dev_p)

    def last_piece(core_of, num, which, first=far):
        return b_v.at[2, pl.ds(first + core_of * GROUP, GROUP), pl.ds(which * half + num * fine, fine)]

    def last_x_send(num):
        return remote(b_ref.at[pl.ds(last * GROUP, GROUP), pl.ds(depth * half + num * fine, fine)],
                      last_piece(core, num, depth, near), send_xl, recv_xl, num, dev_x)

    def last_x_extra(num):
        return remote(b_ref.at[pl.ds(last * GROUP, GROUP), pl.ds((1 - depth) * half + num * fine, fine)],
                      last_piece(core, num, 1 - depth, near), send_zl, recv_zl, num, dev_x)

    def last_x_recv(num):
        here = last_piece(core, num, depth)
        return remote(here, here, send_xl, recv_xl, num, dev_x)

    def last_z_send(num):
        here = last_piece(core, num, depth)
        return remote(here, here, send_zl, recv_zl, num, dev_z)

    def last_z_recv(num):
        here = last_piece(core, num, 1 - depth)
        return remote(here, here, send_zl, recv_zl, num, dev_z)

    def last_px_send(num):
        here = last_piece(core, num, depth)
        return remote(here, here, send_pxl, recv_pxl, num, dev_p)

    def last_px_recv(num):
        here = last_piece(1 - core, num, depth)
        return remote(here, here, send_pxl, recv_pxl, num, dev_p)

    def last_pz_send(num):
        here = last_piece(core, num, 1 - depth)
        return remote(here, here, send_pzl, recv_pzl, num, dev_p)

    def last_pz_recv(num):
        here = last_piece(1 - core, num, 1 - depth)
        return remote(here, here, send_pzl, recv_pzl, num, dev_p)

    def own_send(step):
        return remote(
            b_ref.at[pl.ds(step * GROUP, GROUP), :], ball.at[pl.ds(row * band + step * GROUP, GROUP), :],
            send_own, recv_own, step, dev_p)

    def own_recv(step):
        here = ball.at[pl.ds(row_peer * band + step * GROUP, GROUP), :]
        return remote(here, here, send_own, recv_own, step, dev_p)

    def near_loads(step, slot):
        pltpu.make_async_copy(
            b_ref.at[pl.ds(step * GROUP, GROUP), :],
            b_v.at[slot, pl.ds(near + core * GROUP, GROUP), :], load_near.at[lax.rem(step, 2)]).start()
        pltpu.make_async_copy(
            ball.at[pl.ds(row_peer * band + step * GROUP, GROUP), :],
            b_v.at[slot, pl.ds(near + (1 - core) * GROUP, GROUP), :], load_near.at[lax.rem(step, 2)]).start()

    def near_wait(step, slot):
        here = b_v.at[slot, pl.ds(near, 2 * GROUP), :]
        pltpu.make_async_copy(here, here, load_near.at[lax.rem(step, 2)]).wait()

    def tile_cols(num):
        at = lax.rem(num, 2 * tiles)
        which = jnp.where(at < tiles, depth, 1 - depth)
        return pl.ds(pl.multiple_of(which * half + lax.rem(at, tiles) * TILE, TILE), TILE)

    def far_loads(num):
        step = num // SUBS
        slot = slot_of(step)
        at = tile_cols(num)
        for band_row, part in ((row_far, core), (row_far_peer, 1 - core)):
            pltpu.make_async_copy(
                ball.at[pl.ds(band_row * band + step * GROUP, GROUP), at],
                b_v.at[slot, pl.ds(far + part * GROUP, GROUP), at], load_far.at[lax.rem(num, SUBS)]).start()

    def far_wait(num):
        here = b_v.at[slot_of(num // SUBS), pl.ds(far, 2 * GROUP), tile_cols(num)]
        pltpu.make_async_copy(here, here, load_far.at[lax.rem(num, SUBS)]).wait()

    def sent(num):
        x_send(num).wait_send()
        z_send(num).wait_send()
        px_send(num).wait_send()
        pz_send(num).wait_send()

    def start_group(step, slot):
        own_recv(step).wait_recv()
        near_loads(step, slot)

        @pl.when(step + 2 < steps)
        def _():
            own_send(step + 2).start()

        @pl.when(step >= 1)
        def _():
            a_recv(step - 1).wait_recv()
            near_wait(step - 1, slot_of(step - 1))

    def add(step, at):
        acc[:, at] += jnp.dot(a_v[step], b_v[slot_of(step), :, at], preferred_element_type=jnp.float32)

    def load(new):
        at = lax.rem(new, 2 * tiles)
        first = (new // SUBS) * SUBS + lax.rem(at, tiles) * per

        @pl.when(at < tiles)
        def _():
            for k in range(per):
                px_recv(first + k).wait_recv()

        @pl.when(at >= tiles)
        def _():
            for k in range(per):
                pz_recv(first + k).wait_recv()
        far_loads(new)

    barrier = pltpu.get_barrier_semaphore()
    for dev in (dev_x, dev_y, dev_z, dev_p):
        pl.semaphore_signal(barrier, inc=1, device_id=dev, device_id_type=MESH)

    @pl.loop(0, steps)
    def _(step):
        a_load(step, 0).start()
        a_load(step, 1).start()

    pl.semaphore_wait(barrier, 4)

    x_send(0).start()
    a_load_wait(0)
    a_send(0).start()

    @pl.loop(1, AHEAD)
    def _(num):
        x_send(num).start()

    own_send(0).start()
    own_send(1).start()

    @pl.loop(1, steps)
    def _(step):
        a_load_wait(step)
        a_send(step).start()

    @pl.loop(0, cols // TILE)
    def _(tile):
        at = pl.ds(pl.multiple_of(tile * TILE, TILE), TILE)
        acc[:, at] = jnp.zeros((rows_c, TILE), jnp.float32)

    @pl.loop(0, body)
    def _(num):
        step = num // SUBS
        x_recv(num).wait_recv()
        z_send(num).start()
        px_send(num).start()

        @pl.when(num + AHEAD < body)
        def _():
            x_send(num + AHEAD).start()

        @pl.when(num + AHEAD >= body)
        def _():
            for k in range(2):
                new = (num + AHEAD - body) * 2 + k

                @pl.when(new < FINE)
                def _():
                    last_x_send(new).start()

                @pl.when((new >= FINE) & (new < FINE + SHIFT))
                def _():
                    last_x_extra(new - SHIFT).start()

        @pl.when(lax.rem(num, SUBS) == 0)
        def _():
            start_group(step, slot_of(step))

        @pl.when(step >= 1)
        def _():
            far_wait(num - SUBS)
            add(step - 1, tile_cols(num))

        @pl.when(num >= LAG)
        def _():
            z_recv(num - LAG).wait_recv()
            pz_send(num - LAG).start()

        @pl.when(num >= LOAD)
        def _():
            load(num - LOAD)

        @pl.when(num >= BACK)
        def _():
            sent(num - BACK)

        @pl.when((lax.rem(num, SUBS) == 0) & (step >= 2))
        def _():
            a_send(step - 2).wait_send()
            own_send(step - 2).wait_send()

    def relay_out(num):
        last_z_recv(num).wait_recv()
        last_pz_send(num).start()

    for num in range(FINE):
        last_x_recv(num).wait_recv()
        if num < FINE - SHIFT:
            last_z_send(num).start()
        last_px_send(num).start()
        if num == 0:
            start_group(last, 2)
        part = num * SUBS // FINE
        if num % (FINE // SUBS) == 0:
            far_wait(body - SUBS + part)
        which = depth if part < tiles else 1 - depth
        add(last - 1, pl.ds(pl.multiple_of(
            which * half + (part % tiles) * TILE + (num % (FINE // SUBS)) * HALF_TILE, HALF_TILE), HALF_TILE))
        if num in (1, 3):
            z_recv(body - LAG + num // 2).wait_recv()
            pz_send(body - LAG + num // 2).start()
        if num >= FINE_LAG:
            relay_out(num - FINE_LAG)
        if num in LOADS:
            load(body - LOAD + LOADS.index(num))

    def finish(which, first, size):
        at = pl.ds(pl.multiple_of(which * half + first, HALF_TILE), size)
        total = acc[:, at] + jnp.dot(a_v[last], b_v[2, :, at], preferred_element_type=jnp.float32)
        o_v[:, at] = total.astype(o_v.dtype)

    a_recv(last).wait_recv()
    near_wait(last, 2)
    for part in range(2):
        for k in range(FINE // 2):
            last_px_recv(part * FINE // 2 + k).wait_recv()
        finish(depth, part * TILE, TILE)
        relay_out(FINE - FINE_LAG + part)
    for part in range(4):
        for k in range(FINE // 4):
            last_pz_recv(part * FINE // 4 + k).wait_recv()
        finish(1 - depth, part * HALF_TILE, HALF_TILE)
        if part < 2:
            relay_out(FINE - FINE_LAG + 2 + part)

    @pl.loop(body - BACK, body)
    def _(num):
        sent(num)

    @pl.loop(0, FINE)
    def _(num):
        last_x_send(num).wait_send()
        last_z_send(num).wait_send()
        last_px_send(num).wait_send()
        last_pz_send(num).wait_send()

    @pl.loop(steps - 3, steps)
    def _(step):
        a_send(step).wait_send()
        own_send(step).wait_send()


def solution(mesh):
    def local_mm(a_blk, b_blk):
        band, cols = b_blk.shape
        rows_c = a_blk.shape[0] // 2
        steps = band // GROUP
        count = (steps - 1) * SUBS
        any_spec = pl.BlockSpec(memory_space=pl.ANY)
        dma = pltpu.SemaphoreType.DMA
        c_blk, _ = pl.pallas_call(
            kernel,
            out_shape=(pltpu.VMEM((rows_c, cols), jnp.bfloat16),
                       jax.ShapeDtypeStruct((4 * band, cols), jnp.bfloat16)),
            in_specs=[any_spec] * 2,
            out_specs=(pl.BlockSpec(memory_space=pltpu.VMEM), any_spec),
            scratch_shapes=[
                pltpu.VMEM((steps, rows_c, 4 * GROUP), jnp.bfloat16),
                pltpu.VMEM((rows_c, cols), jnp.float32),
                pltpu.VMEM((3, 4 * GROUP, cols), jnp.bfloat16),
                dma((steps,)), dma((steps,)), dma((steps,)),
                dma((count,)), dma((count,)), dma((count,)), dma((count,)),
                dma((steps,)), dma((steps,)),
                dma((count,)), dma((count,)), dma((count,)), dma((count,)),
                dma((SUBS,)), dma((2,)),
                *[dma((FINE,))] * 8,
            ],
            compiler_params=pltpu.CompilerParams(
                collective_id=0, has_side_effects=True, vmem_limit_bytes=52 * 1024 * 1024),
            cost_estimate=pl.CostEstimate(
                flops=2 * rows_c * cols * 2 * cols, bytes_accessed=200 * 2 ** 20, transcendentals=0),
        )(a_blk, b_blk)
        return c_blk

    return jax.shard_map(
        local_mm, mesh=mesh, in_specs=(P("row", "col"), P("row", "col")),
        out_specs=P(("row", "depth"), "col"), check_vma=False)
```

time: 202 us -> 202 us (level)
  no operation moved by 1% of the time
where the time goes in v9:
time: 202 us; the launch traced here: 201 us
  Pallas kernels  198 us (98%)
  local copies, waits for them, and re-layouts  3.4 us (2%)
    pallas_call x1, Pallas kernels, local_mm(): pl.pallas_call(kernel, out_shape=(pltpu.VMEM((rows_c, cols), jnp.bfloat16...  198 us

profile of v9, /device:TPU:0, one launch (start us, length us, event | category | flops | bytes accessed | tf_op | source)
XLA Modules:
  0.0 201.5 jit_solution(1331520493526397564)
XLA Ops:
  0.0 198.0 %shard_map.28 = (bf16[1024,4096]{1,0:T(8,128)(2,1)S(1)}, bf16[8192,4096]{1,0:T(8,128)(2,1)}) custom-call(bf16[2048,4096]{1,0:T(8,128)(2,1)} %a_ref.1, bf16[2048,4096]{1,0:T(8,128)(2,1)} %b_ref.1), custom_call_target="tpu_custom_call" | custom-call | flops 68719476736 | bytes 209715200 | tf_op jit(solution)/shard_map/pallas_call | solution.py:384
  198.1 3.4 %copy.4 = bf16[1024,4096]{1,0:T(8,128)(2,1)} copy(bf16[1024,4096]{1,0:T(8,128)(2,1)S(1)} %get-tuple-element.6) | data formatting | bytes 16777216

commit v10 on v9

--- a/solution.py
+++ b/solution.py
@@ -11,7 +11,7 @@
 AHEAD = 6
 LAG = 2
 FINE = 8
-FINE_LAG = 4
+FINE_LAG = 3
 SHIFT = 2
 LOAD = 3
 TILE = 1024
@@ -233,20 +233,34 @@
     for dev in (dev_x, dev_y, dev_z, dev_p):
         pl.semaphore_signal(barrier, inc=1, device_id=dev, device_id_type=MESH)
 
-    @pl.loop(0, steps)
+    def staged(num):
+        return o_v.at[pl.ds(0, GROUP), pl.ds(num * width, width)]
+
+    def stage(num):
+        return pltpu.make_async_copy(source(num, depth), staged(num), load_far.at[num])
+
+    a_load(0, 0).start()
+    a_load(0, 1).start()
+    for num in range(SUBS):
+        stage(num).start()
+    a_load_wait(0)
+    for num in range(SUBS):
+        stage(num).wait()
+    pl.semaphore_wait(barrier, 4)
+
+    for num in range(SUBS):
+        remote(staged(num), piece(row, num, depth), send_x, recv_x, num, dev_x).start()
+        if num == 0:
+            a_send(0).start()
+
+    @pl.loop(SUBS, AHEAD)
+    def _(num):
+        x_send(num).start()
+
+    @pl.loop(1, steps)
     def _(step):
         a_load(step, 0).start()
         a_load(step, 1).start()
-
-    pl.semaphore_wait(barrier, 4)
-
-    x_send(0).start()
-    a_load_wait(0)
-    a_send(0).start()
-
-    @pl.loop(1, AHEAD)
-    def _(num):
-        x_send(num).start()
 
     own_send(0).start()
     own_send(1).start()
@@ -342,19 +356,16 @@
         total = acc[:, at] + jnp.dot(a_v[last], b_v[2, :, at], preferred_element_type=jnp.float32)
         o_v[:, at] = total.astype(o_v.dtype)
 
+    for num in range(FINE - FINE_LAG, FINE - 1):
+        relay_out(num)
     a_recv(last).wait_recv()
     near_wait(last, 2)
-    for part in range(2):
-        for k in range(FINE // 2):
-            last_px_recv(part * FINE // 2 + k).wait_recv()
-        finish(depth, part * TILE, TILE)
-        relay_out(FINE - FINE_LAG + part)
-    for part in range(4):
-        for k in range(FINE // 4):
-            last_pz_recv(part * FINE // 4 + k).wait_recv()
-        finish(1 - depth, part * HALF_TILE, HALF_TILE)
-        if part < 2:
-            relay_out(FINE - FINE_LAG + 2 + part)
+    for part in range(2 * tiles):
+        for k in range(FINE // tiles):
+            (last_px_recv if part < tiles else last_pz_recv)(part % tiles * FINE // tiles + k).wait_recv()
+        finish(depth if part < tiles else 1 - depth, part % tiles * TILE, TILE)
+        if part == 0:
+            relay_out(FINE - 1)
 
     @pl.loop(body - BACK, body)
     def _(num):

time: 202 us -> 202 us (level)
  no operation moved by 1% of the time
where the time goes in v10:
time: 202 us
  Pallas kernels  199 us (99%)
  local copies, waits for them, and re-layouts  3.4 us (2%)
    pallas_call x1, Pallas kernels, local_mm(): pl.pallas_call(kernel, out_shape=(pltpu.VMEM((rows_c, cols), jnp.bfloat16...  199 us

profile of v10, /device:TPU:0, one launch (start us, length us, event | category | flops | bytes accessed | tf_op | source)
XLA Modules:
  0.0 202.1 jit_solution(10726482474048044607)
XLA Ops:
  0.0 198.6 %shard_map.28 = (bf16[1024,4096]{1,0:T(8,128)(2,1)S(1)}, bf16[8192,4096]{1,0:T(8,128)(2,1)}) custom-call(bf16[2048,4096]{1,0:T(8,128)(2,1)} %a_ref.1, bf16[2048,4096]{1,0:T(8,128)(2,1)} %b_ref.1), custom_call_target="tpu_custom_call" | custom-call | flops 68719476736 | bytes 209715200 | tf_op jit(solution)/shard_map/pallas_call | solution.py:395
  198.7 3.4 %copy.4 = bf16[1024,4096]{1,0:T(8,128)(2,1)} copy(bf16[1024,4096]{1,0:T(8,128)(2,1)S(1)} %get-tuple-element.6) | data formatting | bytes 16777216

commit v11 on v10

--- a/solution.py
+++ b/solution.py
@@ -265,16 +265,6 @@
     own_send(0).start()
     own_send(1).start()
 
-    @pl.loop(1, steps)
-    def _(step):
-        a_load_wait(step)
-        a_send(step).start()
-
-    @pl.loop(0, cols // TILE)
-    def _(tile):
-        at = pl.ds(pl.multiple_of(tile * TILE, TILE), TILE)
-        acc[:, at] = jnp.zeros((rows_c, TILE), jnp.float32)
-
     @pl.loop(0, body)
     def _(num):
         step = num // SUBS
@@ -299,9 +289,23 @@
                 def _():
                     last_x_extra(new - SHIFT).start()
 
+        @pl.when((num == 0) | (num == 1))
+        def _():
+            a_load_wait(num + 1)
+            a_send(num + 1).start()
+
+        @pl.when((lax.rem(num, SUBS) == 0) & (step >= 1) & (step + 2 < steps))
+        def _():
+            a_load_wait(step + 2)
+            a_send(step + 2).start()
+
         @pl.when(lax.rem(num, SUBS) == 0)
         def _():
             start_group(step, slot_of(step))
+
+        @pl.when(step == 0)
+        def _():
+            acc[:, tile_cols(num)] = jnp.zeros((rows_c, TILE), jnp.float32)
 
         @pl.when(step >= 1)
         def _():

time: 202 us -> 202 us (level)
  no operation moved by 1% of the time
where the time goes in v11:
time: 202 us
  Pallas kernels  199 us (99%)
  local copies, waits for them, and re-layouts  3.4 us (2%)
    pallas_call x1, Pallas kernels, local_mm(): pl.pallas_call(kernel, out_shape=(pltpu.VMEM((rows_c, cols), jnp.bfloat16...  199 us

profile of v11, /device:TPU:0, one launch (start us, length us, event | category | flops | bytes accessed | tf_op | source)
XLA Modules:
  0.0 202.1 jit_solution(8505980815243513141)
XLA Ops:
  0.0 198.6 %shard_map.28 = (bf16[1024,4096]{1,0:T(8,128)(2,1)S(1)}, bf16[8192,4096]{1,0:T(8,128)(2,1)}) custom-call(bf16[2048,4096]{1,0:T(8,128)(2,1)} %a_ref.1, bf16[2048,4096]{1,0:T(8,128)(2,1)} %b_ref.1), custom_call_target="tpu_custom_call" | custom-call | flops 68719476736 | bytes 209715200 | tf_op jit(solution)/shard_map/pallas_call | solution.py:399
  198.7 3.4 %copy.4 = bf16[1024,4096]{1,0:T(8,128)(2,1)} copy(bf16[1024,4096]{1,0:T(8,128)(2,1)S(1)} %get-tuple-element.6) | data formatting | bytes 16777216

commit v12 on v11

--- a/solution.py
+++ b/solution.py
@@ -233,27 +233,15 @@
     for dev in (dev_x, dev_y, dev_z, dev_p):
         pl.semaphore_signal(barrier, inc=1, device_id=dev, device_id_type=MESH)
 
-    def staged(num):
-        return o_v.at[pl.ds(0, GROUP), pl.ds(num * width, width)]
-
-    def stage(num):
-        return pltpu.make_async_copy(source(num, depth), staged(num), load_far.at[num])
-
     a_load(0, 0).start()
     a_load(0, 1).start()
-    for num in range(SUBS):
-        stage(num).start()
+    pl.semaphore_wait(barrier, 4)
+    x_send(0).start()
+    x_send(1).start()
     a_load_wait(0)
-    for num in range(SUBS):
-        stage(num).wait()
-    pl.semaphore_wait(barrier, 4)
-
-    for num in range(SUBS):
-        remote(staged(num), piece(row, num, depth), send_x, recv_x, num, dev_x).start()
-        if num == 0:
-            a_send(0).start()
-
-    @pl.loop(SUBS, AHEAD)
+    a_send(0).start()
+
+    @pl.loop(2, AHEAD)
     def _(num):
         x_send(num).start()
 

time: 202 us -> 202 us (level)
  no operation moved by 1% of the time
where the time goes in v12:
time: 202 us
  Pallas kernels  199 us (99%)
  local copies, waits for them, and re-layouts  3.4 us (2%)
    pallas_call x1, Pallas kernels, local_mm(): pl.pallas_call(kernel, out_shape=(pltpu.VMEM((rows_c, cols), jnp.bfloat16...  199 us

profile of v12, /device:TPU:0, one launch (start us, length us, event | category | flops | bytes accessed | tf_op | source)
XLA Modules:
  0.0 202.1 jit_solution(8307094992210142512)
XLA Ops:
  0.0 198.6 %shard_map.28 = (bf16[1024,4096]{1,0:T(8,128)(2,1)S(1)}, bf16[8192,4096]{1,0:T(8,128)(2,1)}) custom-call(bf16[2048,4096]{1,0:T(8,128)(2,1)} %a_ref.1, bf16[2048,4096]{1,0:T(8,128)(2,1)} %b_ref.1), custom_call_target="tpu_custom_call" | custom-call | flops 68719476736 | bytes 209715200 | tf_op jit(solution)/shard_map/pallas_call | solution.py:387
  198.7 3.4 %copy.4 = bf16[1024,4096]{1,0:T(8,128)(2,1)} copy(bf16[1024,4096]{1,0:T(8,128)(2,1)S(1)} %get-tuple-element.6) | data formatting | bytes 16777216

commit v13 on v12

--- a/solution.py
+++ b/solution.py
@@ -16,6 +16,7 @@
 LOAD = 3
 TILE = 1024
 BACK = 8
+EARLY = 768
 HALF_TILE = 512
 LOADS = (0, 2, 5)
 
@@ -23,7 +24,8 @@
 def kernel(a_ref, b_ref, o_v, ball, a_v, acc, b_v,
            load_a, send_a, recv_a, send_x, recv_x, send_z, recv_z, send_own, recv_own,
            send_px, recv_px, send_pz, recv_pz, load_far, load_near,
-           send_xl, recv_xl, send_zl, recv_zl, send_pxl, recv_pxl, send_pzl, recv_pzl):
+           send_xl, recv_xl, send_zl, recv_zl, send_pxl, recv_pxl, send_pzl, recv_pzl,
+           send_al, recv_al):
     depth = lax.axis_index("depth")
     col = lax.axis_index("col")
     row = lax.axis_index("row")
@@ -40,6 +42,7 @@
     body = last * SUBS
     per = TILE // width
     tiles = half // TILE
+    row_parts = ((0, EARLY), (EARLY, rows_c - EARLY))
 
     row_far = lax.rem(row + 2, 4)
     row_peer = chip_x * 2 + (1 - core)
@@ -75,6 +78,10 @@
     def a_recv(step):
         return remote(a_cols(step, 1 - col), a_cols(step, 1 - col), send_a, recv_a, step, dev_y)
 
+    def last_a(part, side):
+        here = a_v.at[last, pl.ds(*row_parts[part]), pl.ds(side * 2 * GROUP, 2 * GROUP)]
+        return remote(here, here, send_al, recv_al, part, dev_y)
+
     def piece(band_row, num, which):
         return ball.at[pl.ds(band_row * band + (num // SUBS) * GROUP, GROUP),
                        pl.ds(which * half + lax.rem(num, SUBS) * width, width)]
@@ -285,7 +292,15 @@
         @pl.when((lax.rem(num, SUBS) == 0) & (step >= 1) & (step + 2 < steps))
         def _():
             a_load_wait(step + 2)
-            a_send(step + 2).start()
+
+            @pl.when(step + 2 < last)
+            def _():
+                a_send(step + 2).start()
+
+            @pl.when(step + 2 == last)
+            def _():
+                for part in range(2):
+                    last_a(part, col).start()
 
         @pl.when(lax.rem(num, SUBS) == 0)
         def _():
@@ -343,21 +358,31 @@
         if num in LOADS:
             load(body - LOAD + LOADS.index(num))
 
-    def finish(which, first, size):
-        at = pl.ds(pl.multiple_of(which * half + first, HALF_TILE), size)
-        total = acc[:, at] + jnp.dot(a_v[last], b_v[2, :, at], preferred_element_type=jnp.float32)
-        o_v[:, at] = total.astype(o_v.dtype)
+    def finish(tile, first, size):
+        which = depth if tile < tiles else 1 - depth
+        at = pl.ds(pl.multiple_of(which * half + tile % tiles * TILE, TILE), TILE)
+        rows = pl.ds(first, size)
+        total = acc[rows, at] + jnp.dot(a_v[last, rows, :], b_v[2, :, at], preferred_element_type=jnp.float32)
+        o_v[rows, at] = total.astype(o_v.dtype)
+
+    def wait_tile(tile):
+        for k in range(FINE // tiles):
+            (last_px_recv if tile < tiles else last_pz_recv)(tile % tiles * FINE // tiles + k).wait_recv()
 
     for num in range(FINE - FINE_LAG, FINE - 1):
         relay_out(num)
-    a_recv(last).wait_recv()
+    last_a(0, 1 - col).wait_recv()
     near_wait(last, 2)
-    for part in range(2 * tiles):
-        for k in range(FINE // tiles):
-            (last_px_recv if part < tiles else last_pz_recv)(part % tiles * FINE // tiles + k).wait_recv()
-        finish(depth if part < tiles else 1 - depth, part % tiles * TILE, TILE)
-        if part == 0:
+    for tile in range(2 * tiles - 1):
+        wait_tile(tile)
+        finish(tile, *row_parts[0])
+        if tile == 0:
             relay_out(FINE - 1)
+    last_a(1, 1 - col).wait_recv()
+    for tile in range(2 * tiles - 1):
+        finish(tile, *row_parts[1])
+    wait_tile(2 * tiles - 1)
+    finish(2 * tiles - 1, 0, rows_c)
 
     @pl.loop(body - BACK, body)
     def _(num):
@@ -370,9 +395,15 @@
         last_px_send(num).wait_send()
         last_pz_send(num).wait_send()
 
+    for part in range(2):
+        last_a(part, col).wait_send()
+
+    @pl.loop(steps - 3, last)
+    def _(step):
+        a_send(step).wait_send()
+
     @pl.loop(steps - 3, steps)
     def _(step):
-        a_send(step).wait_send()
         own_send(step).wait_send()
 
 
@@ -400,6 +431,7 @@
                 dma((count,)), dma((count,)), dma((count,)), dma((count,)),
                 dma((SUBS,)), dma((2,)),
                 *[dma((FINE,))] * 8,
+                dma((2,)), dma((2,)),
             ],
             compiler_params=pltpu.CompilerParams(
                 collective_id=0, has_side_effects=True, vmem_limit_bytes=52 * 1024 * 1024),

time: 202 us -> 203 us (level)
  no operation moved by 1% of the time
where the time goes in v13:
time: 203 us; the launch traced here: 202 us
  Pallas kernels  199 us (98%)
  local copies, waits for them, and re-layouts  3.4 us (2%)
    pallas_call x1, Pallas kernels, local_mm(): pl.pallas_call(kernel, out_shape=(pltpu.VMEM((rows_c, cols), jnp.bfloat16...  199 us

profile of v13, /device:TPU:0, one launch (start us, length us, event | category | flops | bytes accessed | tf_op | source)
XLA Modules:
  0.0 202.3 jit_solution(16116310671348986931)
XLA Ops:
  0.0 198.9 %shard_map.28 = (bf16[1024,4096]{1,0:T(8,128)(2,1)S(1)}, bf16[8192,4096]{1,0:T(8,128)(2,1)}) custom-call(bf16[2048,4096]{1,0:T(8,128)(2,1)} %a_ref.1, bf16[2048,4096]{1,0:T(8,128)(2,1)} %b_ref.1), custom_call_target="tpu_custom_call" | custom-call | flops 68719476736 | bytes 209715200 | tf_op jit(solution)/shard_map/pallas_call | solution.py:418
  198.9 3.4 %copy.4 = bf16[1024,4096]{1,0:T(8,128)(2,1)} copy(bf16[1024,4096]{1,0:T(8,128)(2,1)S(1)} %get-tuple-element.6) | data formatting | bytes 16777216

commit v14 on v12

--- a/solution.py
+++ b/solution.py
@@ -11,13 +11,15 @@
 AHEAD = 6
 LAG = 2
 FINE = 8
-FINE_LAG = 3
+FINE_LAG = 6
 SHIFT = 2
-LOAD = 3
+LOAD = 4
+FAR = 6
 TILE = 1024
 BACK = 8
 HALF_TILE = 512
-LOADS = (0, 2, 5)
+LOADS = (0, 1, 2, 5)
+DOTS = (0, 1, 2, 3, 4, 7)
 
 
 def kernel(a_ref, b_ref, o_v, ball, a_v, acc, b_v,
@@ -206,10 +208,9 @@
         def _():
             own_send(step + 2).start()
 
-        @pl.when(step >= 1)
-        def _():
-            a_recv(step - 1).wait_recv()
-            near_wait(step - 1, slot_of(step - 1))
+    def meet(step):
+        a_recv(step).wait_recv()
+        near_wait(step, slot_of(step))
 
     def add(step, at):
         acc[:, at] += jnp.dot(a_v[step], b_v[slot_of(step), :, at], preferred_element_type=jnp.float32)
@@ -287,18 +288,23 @@
             a_load_wait(step + 2)
             a_send(step + 2).start()
 
-        @pl.when(lax.rem(num, SUBS) == 0)
+        @pl.when(step == 0)
+        def _():
+            acc[:, tile_cols(num)] = jnp.zeros((rows_c, TILE), jnp.float32)
+
+        @pl.when(num >= FAR)
+        def _():
+            new = num - FAR
+
+            @pl.when(lax.rem(new, SUBS) == 0)
+            def _():
+                meet(new // SUBS)
+            far_wait(new)
+            add(new // SUBS, tile_cols(new))
+
+        @pl.when(lax.rem(num, SUBS) == FAR - SUBS)
         def _():
             start_group(step, slot_of(step))
-
-        @pl.when(step == 0)
-        def _():
-            acc[:, tile_cols(num)] = jnp.zeros((rows_c, TILE), jnp.float32)
-
-        @pl.when(step >= 1)
-        def _():
-            far_wait(num - SUBS)
-            add(step - 1, tile_cols(num))
 
         @pl.when(num >= LAG)
         def _():
@@ -327,14 +333,14 @@
         if num < FINE - SHIFT:
             last_z_send(num).start()
         last_px_send(num).start()
-        if num == 0:
+        if num in DOTS:
+            new = body - FAR + DOTS.index(num)
+            if new % SUBS == 0:
+                meet(last - 1)
+            far_wait(new)
+            add(new // SUBS, tile_cols(new))
+        if num == 1:
             start_group(last, 2)
-        part = num * SUBS // FINE
-        if num % (FINE // SUBS) == 0:
-            far_wait(body - SUBS + part)
-        which = depth if part < tiles else 1 - depth
-        add(last - 1, pl.ds(pl.multiple_of(
-            which * half + (part % tiles) * TILE + (num % (FINE // SUBS)) * HALF_TILE, HALF_TILE), HALF_TILE))
         if num in (1, 3):
             z_recv(body - LAG + num // 2).wait_recv()
             pz_send(body - LAG + num // 2).start()
@@ -348,16 +354,29 @@
         total = acc[:, at] + jnp.dot(a_v[last], b_v[2, :, at], preferred_element_type=jnp.float32)
         o_v[:, at] = total.astype(o_v.dtype)
 
-    for num in range(FINE - FINE_LAG, FINE - 1):
-        relay_out(num)
+    def direct(part):
+        for k in range(FINE // tiles):
+            last_px_recv(part * FINE // tiles + k).wait_recv()
+        finish(depth, part * TILE, TILE)
+
+    def relayed(first, size):
+        for k in range(size // fine):
+            last_pz_recv(first // fine + k).wait_recv()
+        finish(1 - depth, first, size)
+
+    relay_out(2)
+    relay_out(3)
+    relay_out(6)
     a_recv(last).wait_recv()
     near_wait(last, 2)
-    for part in range(2 * tiles):
-        for k in range(FINE // tiles):
-            (last_px_recv if part < tiles else last_pz_recv)(part % tiles * FINE // tiles + k).wait_recv()
-        finish(depth if part < tiles else 1 - depth, part % tiles * TILE, TILE)
-        if part == 0:
-            relay_out(FINE - 1)
+    direct(0)
+    relay_out(7)
+    relay_out(4)
+    direct(1)
+    relay_out(5)
+    relayed(0, TILE)
+    relayed(TILE + HALF_TILE, HALF_TILE)
+    relayed(TILE, HALF_TILE)
 
     @pl.loop(body - BACK, body)
     def _(num):

time: 202 us -> 202 us (level)
  no operation moved by 1% of the time
where the time goes in v14:
time: 202 us
  Pallas kernels  198 us (98%)
  local copies, waits for them, and re-layouts  3.4 us (2%)
    pallas_call x1, Pallas kernels, local_mm(): pl.pallas_call(kernel, out_shape=(pltpu.VMEM((rows_c, cols), jnp.bfloat16...  198 us

profile of v14, /device:TPU:0, one launch (start us, length us, event | category | flops | bytes accessed | tf_op | source)
XLA Modules:
  0.0 201.8 jit_solution(514001621002837584)
XLA Ops:
  0.0 198.4 %shard_map.28 = (bf16[1024,4096]{1,0:T(8,128)(2,1)S(1)}, bf16[8192,4096]{1,0:T(8,128)(2,1)}) custom-call(bf16[2048,4096]{1,0:T(8,128)(2,1)} %a_ref.1, bf16[2048,4096]{1,0:T(8,128)(2,1)} %b_ref.1), custom_call_target="tpu_custom_call" | custom-call | flops 68719476736 | bytes 209715200 | tf_op jit(solution)/shard_map/pallas_call | solution.py:406
  198.4 3.4 %copy.4 = bf16[1024,4096]{1,0:T(8,128)(2,1)} copy(bf16[1024,4096]{1,0:T(8,128)(2,1)S(1)} %get-tuple-element.6) | data formatting | bytes 16777216

commit v15 on v8

--- a/solution.py
+++ b/solution.py
@@ -335,6 +335,19 @@
     def _(step):
         a_send(step).wait_send()
         own_send(step).wait_send()
+
+
+CHUNKS = 8
+
+
+def write_out(done, c_ref, sems):
+    rows = done.shape[0] // CHUNKS
+    copies = [pltpu.make_async_copy(done.at[pl.ds(k * rows, rows)], c_ref.at[pl.ds(k * rows, rows)], sems.at[k])
+              for k in range(CHUNKS)]
+    for copy in copies:
+        copy.start()
+    for copy in copies:
+        copy.wait()
 
 
 def solution(mesh):
@@ -366,7 +379,14 @@
             cost_estimate=pl.CostEstimate(
                 flops=2 * rows_c * cols * 2 * cols, bytes_accessed=200 * 2 ** 20, transcendentals=0),
         )(a_blk, b_blk)
-        return c_blk
+        return pl.pallas_call(
+            write_out,
+            out_shape=jax.ShapeDtypeStruct((rows_c, cols), jnp.bfloat16),
+            in_specs=[pl.BlockSpec(memory_space=pltpu.VMEM)],
+            out_specs=any_spec,
+            scratch_shapes=[dma((CHUNKS,))],
+            compiler_params=pltpu.CompilerParams(vmem_limit_bytes=1024 * 1024),
+        )(pltpu.with_memory_space_constraint(c_blk, pltpu.VMEM))
 
     return jax.shard_map(
         local_mm, mesh=mesh, in_specs=(P("row", "col"), P("row", "col")),

time: 202 us -> 202 us (level)
  local copies, waits for them, and re-layouts: 3.4 us -> 0 us
  Pallas kernels: 198 us -> 201 us
    unnamed x1 -> x0, local copies, waits for them, and re-layouts: 3.4 us -> none
    pallas_call x0 -> x1, Pallas kernels: none -> 3.37 us  [local_mm(): pl.pallas_call(write_out, out_shape=jax.ShapeDtypeStruct((rows_c, cols),...]
where the time goes in v15:
time: 202 us; the launch traced here: 201 us
  Pallas kernels  201 us (100%)
    pallas_call x1, Pallas kernels, local_mm(): pl.pallas_call(kernel, out_shape=(pltpu.VMEM((rows_c, cols), jnp.bfloat16...  198 us

profile of v15, /device:TPU:0, one launch (start us, length us, event | category | flops | bytes accessed | tf_op | source)
XLA Modules:
  0.0 201.3 jit_solution(17575480074408075590)
XLA Ops:
  0.0 197.9 %shard_map.28 = (bf16[1024,4096]{1,0:T(8,128)(2,1)S(1)}, bf16[8192,4096]{1,0:T(8,128)(2,1)}) custom-call(bf16[2048,4096]{1,0:T(8,128)(2,1)} %a_ref.1, bf16[2048,4096]{1,0:T(8,128)(2,1)} %b_ref.1), custom_call_target="tpu_custom_call" | custom-call | flops 68719476736 | bytes 209715200 | tf_op jit(solution)/shard_map/pallas_call | solution.py:361
  197.9 3.4 %shard_map.29 = bf16[1024,4096]{1,0:T(8,128)(2,1)} custom-call(bf16[1024,4096]{1,0:T(8,128)(2,1)S(1)} %get-tuple-element.6.done), custom_call_target="tpu_custom_call" | custom-call | tf_op jit(solution)/shard_map/pallas_call | solution.py:382

commit v16 on v15

--- a/solution.py
+++ b/solution.py
@@ -306,22 +306,26 @@
         z_recv(num, True).wait_recv()
         pz_send(num, True).start()
 
+    def finish(part, first, size):
+        which = depth if part < wide else 1 - depth
+        at = pl.ds(pl.multiple_of(which * half + part % wide * WIDE + first, size), size)
+        total = acc[:, at] + jnp.dot(a_v[last], b_v[2, :, at], preferred_element_type=jnp.float32)
+        o_v[:, at] = total.astype(o_v.dtype)
+
     a_recv(last).wait_recv()
     near_wait(last, 2)
     wide = half // WIDE
-    for part in range(2 * wide):
-        which = depth if part < wide else 1 - depth
-        first = (part % wide) * (WIDE // width)
+    for part in range(wide):
         for k in range(WIDE // width):
-            if part < wide:
-                px_recv(body + first + k, True).wait_recv()
-            else:
-                pz_recv(body + first + k, True).wait_recv()
-        at = pl.ds(pl.multiple_of(which * half + (part % wide) * WIDE, WIDE), WIDE)
-        total = acc[:, at] + jnp.dot(a_v[last], b_v[2, :, at], preferred_element_type=jnp.float32)
-        o_v[:, at] = total.astype(o_v.dtype)
-        if part < LAG:
-            relay_out(count - LAG + part)
+            px_recv(body + part * (WIDE // width) + k, True).wait_recv()
+        finish(part, 0, WIDE)
+        relay_out(count - 1 - part)
+    for k in range(2):
+        pz_recv(body + k, True).wait_recv()
+    finish(wide, 0, WIDE)
+    for k in (1, 0):
+        pz_recv(body + 2 + k, True).wait_recv()
+        finish(wide + 1, k * width, width)
 
     @pl.loop(count - BACK, body)
     def _(num):

time: 202 us -> 202 us (level)
  no operation moved by 1% of the time
where the time goes in v16:
time: 202 us; the launch traced here: 201 us
  Pallas kernels  201 us (100%)
    pallas_call x1, Pallas kernels, local_mm(): pl.pallas_call(kernel, out_shape=(pltpu.VMEM((rows_c, cols), jnp.bfloat16...  198 us

profile of v16, /device:TPU:0, one launch (start us, length us, event | category | flops | bytes accessed | tf_op | source)
XLA Modules:
  0.0 201.5 jit_solution(11684708958182170111)
XLA Ops:
  0.0 198.1 %shard_map.28 = (bf16[1024,4096]{1,0:T(8,128)(2,1)S(1)}, bf16[8192,4096]{1,0:T(8,128)(2,1)}) custom-call(bf16[2048,4096]{1,0:T(8,128)(2,1)} %a_ref.1, bf16[2048,4096]{1,0:T(8,128)(2,1)} %b_ref.1), custom_call_target="tpu_custom_call" | custom-call | flops 68719476736 | bytes 209715200 | tf_op jit(solution)/shard_map/pallas_call | solution.py:365
  198.1 3.4 %shard_map.29 = bf16[1024,4096]{1,0:T(8,128)(2,1)} custom-call(bf16[1024,4096]{1,0:T(8,128)(2,1)S(1)} %get-tuple-element.6.done), custom_call_target="tpu_custom_call" | custom-call | tf_op jit(solution)/shard_map/pallas_call | solution.py:386
